TPU v7x, 256 devices: a whole 4x4x8 slice. The times are simulated.
256 devices in a mesh: slab: 32 (over z, y), rays: 8 (over x, core).
Axes of the slice: x: 4, y: 4, z: 8, core: 2. Of those that a mesh axis runs over, the one named last changes fastest.
Arguments:
- geometry: float32 [6, 8, 512], P(None, 'rays'), may hold values from -1 to 1
- entry: int32 [32, 8, 512], P('slab', 'rays'), may hold values from 0 to 255
- counts: int32 [32, 8, 512], P('slab', 'rays'), may hold values from 0 to 8
- targets: float32 [3, 8, 512], P(None, 'rays', 'slab'), may hold values from 0 to 1
- w_in: float32 [32, 256, 256], P('slab'), may hold values from -0.375 to 0.375
- w_mid: float32 [32, 2, 256, 256], P('slab'), may hold values from -0.375 to 0.375
- w_out: float32 [32, 4, 256], P('slab'), may hold values from -0.375 to 0.375
- b_hid: float32 [32, 3, 256], P('slab'), may hold values from -3 to 3
- b_out: float32 [32, 4], P('slab'), may hold values from -3 to 3
- freqs: float32 [32, 3, 128], P('slab'), may hold values from -3 to 3
Outputs:
- pixels: float32 [3, 8, 512], P(None, 'rays', 'slab')
- grad_in: float32 [32, 256, 256], P('slab')
- grad_mid: float32 [32, 2, 256, 256], P('slab')
- grad_out: float32 [32, 4, 256], P('slab')
- grad_hid: float32 [32, 3, 256], P('slab')
- grad_bout: float32 [32, 4], P('slab')
Inputs may be any that keep to these rules, and one draw needn't show every extreme that they name: `entry`: the index of a ray's first sample in a slab. `counts`: how many of the 8 slots of a ray lie inside a slab; 0 where the ray misses it.
All inputs are finite; a program needn't handle non-finite values.
Results may differ from a plain program's by a relative error of at most 0.0003.
Values sent between devices are 32-bit elements; how exact they have to be, the bound alone decides.
No kernel may reach another device: no remote copies, remote signals or barrier semaphores. Data moves between devices by JAX's collectives and lax.ppermute only.
A program may use at most 128 MiB of HBM per device.

v0:
```python
import math

import jax
import jax.numpy as jnp
from jax import lax
from jax.experimental import pallas as pl
from jax.experimental.pallas import tpu as pltpu
from jax.sharding import PartitionSpec as P

H = 256
FE = 128
SAMP = 8
RAYS = 512
OWN = 16
ROWS = 17
SPB = 2
STEPS = SAMP // SPB
F32 = jnp.float32
BF16 = jnp.bfloat16
NT = (((1,), (1,)), ((), ()))


def mm(a, b):
    return jnp.dot(a, b, preferred_element_type=F32)


def mm_nt(a, b):
    return lax.dot_general(a, b, NT, preferred_element_type=F32)


def split(x):
    hi = x.astype(BF16)
    return hi, (x - hi.astype(F32)).astype(BF16)


def sincos(phase):
    turns = jnp.floor(phase * F32(2.0 / math.pi) + F32(0.5))
    r = phase - turns * F32(1.5703125)
    r = r - turns * F32(4.837512969970703125e-4)
    r = r - turns * F32(7.54978995489188216e-8)
    z = r * r
    s = r + r * z * (F32(-1.6666654611e-1) + z * (F32(8.3321608736e-3) + z * F32(-1.9515295891e-4)))
    c = F32(1.0) - F32(0.5) * z + z * z * (
        F32(4.166664568298827e-2) + z * (F32(-1.388731625493765e-3) + z * F32(2.443315711809948e-5))
    )
    k = turns.astype(jnp.int32)
    odd = (k & 1) == 1
    sine = jnp.where(odd, c, s)
    cosine = jnp.where(odd, s, c)
    sine = jnp.where((k & 2) == 2, -sine, sine)
    cosine = jnp.where(((k + 1) & 2) == 2, -cosine, cosine)
    return sine, cosine


def softplus(x):
    u = jnp.exp(-jnp.abs(x))
    w = F32(1.0) + u
    return jnp.maximum(x, F32(0.0)) + (jnp.log(w) + (u - (w - F32(1.0))))


def sigmoid(x):
    u = jnp.exp(-jnp.abs(x))
    return jnp.where(x >= 0, F32(1.0), u) / (F32(1.0) + u)


def column(row):
    return jnp.broadcast_to(row, (8, row.shape[1])).T[:, 0:1]


def forward_kernel(
    me_ref, geo_ref, entry_ref, counts_ref, tgt_ref, win_ref, wmid_ref, wout_ref, bhid_ref, bout_ref, freqs_ref,
    send_ref, out_ref, fh_ref, fl_ref, h1h_ref, h1l_ref, h2h_ref, h2l_ref, h3h_ref, h3l_ref, s1_ref, s2_ref, s3_ref,
    wh, wl, wo, bias, rot, feat, before, color,
    *, delta,
):
    step = pl.program_id(0)

    @pl.when(step == 0)
    def _():
        for i in range(3):
            w = win_ref[0] if i == 0 else wmid_ref[0, i - 1]
            hi, lo = split(w.T)
            wh[i] = hi
            wl[i] = lo
            bias[i] = jnp.broadcast_to(column(bhid_ref[0, i : i + 1, :]), (H, 128))
        w8 = jnp.concatenate([wout_ref[0], jnp.zeros((4, H), F32)], axis=0)
        hi, lo = split(w8)
        wo[...] = jnp.concatenate([hi.astype(F32), lo.astype(F32)], axis=0).astype(BF16)
        ft = jnp.concatenate([freqs_ref[0], jnp.zeros((5, FE), F32)], axis=0).T
        geo = geo_ref[:, 0, :]
        a = ft[:, 0:1] * geo[0:1] + ft[:, 1:2] * geo[1:2] + ft[:, 2:3] * geo[2:3]
        d = ft[:, 0:1] * geo[3:4] + ft[:, 1:2] * geo[4:5] + ft[:, 2:3] * geo[5:6]
        t0 = F32(0.25) * (entry_ref[0].astype(F32) + F32(0.5))
        s, c = sincos(a + t0 * d)
        feat[0:FE] = s
        feat[FE:] = c
        s, c = sincos(F32(0.25) * d)
        rot[0:FE] = s
        rot[FE:] = c
        before[...] = jnp.zeros_like(before)
        color[...] = jnp.zeros_like(color)

    def slot_input(j):
        s, c = feat[0:FE], feat[FE:]
        fh_ref[j, 0:FE], fl_ref[j, 0:FE] = split(s)
        fh_ref[j, FE:], fl_ref[j, FE:] = split(c)
        rs, rc = rot[0:FE], rot[FE:]
        feat[0:FE] = s * rc + c * rs
        feat[FE:] = c * rc - s * rs

    for j in range(SPB):
        slot_input(j)
    srcs = [(fh_ref, fl_ref), (h1h_ref, h1l_ref), (h2h_ref, h2l_ref), (h3h_ref, h3l_ref)]
    sigs = [s1_ref, s2_ref, s3_ref]
    parts = [(j, k) for j in range(SPB) for k in range(2)]
    for i in range(3):
        b = bias[i, :, 0:1]
        for j, k in parts:
            lanes = slice(256 * k, 256 * k + 256)
            hi = srcs[i][0][j, :, lanes]
            lo = srcs[i][1][j, :, lanes]
            x = mm(wh[i], hi) + mm(wh[i], lo) + mm(wl[i], hi) + b
            h = softplus(x)
            sigs[i][j, :, lanes] = jnp.exp(x - h)
            srcs[i + 1][0][j, :, lanes], srcs[i + 1][1][j, :, lanes] = split(h)
    bo = jnp.concatenate([bout_ref[0:1, :], jnp.zeros((1, 124), F32)], axis=1)
    bo = jnp.broadcast_to(bo, (128, 128)).T[0:8, 0:1]
    for j in range(SPB):
        d1 = mm(wo[...], h3h_ref[j])
        d2 = mm(wo[...], h3l_ref[j])
        o = d1[0:8] + d1[8:16] + d2[0:8] + d2[8:16] + bo
        out_ref[j] = o
        alive = step * SPB + j < counts_ref[0]
        depth = jnp.where(alive, softplus(o[0:1]) * F32(delta), F32(0.0))
        bef = before[...]
        w = jnp.exp(-bef) * (F32(1.0) - jnp.exp(-depth))
        color[...] += w * sigmoid(o)
        before[...] = bef + depth

    @pl.when(step == STEPS - 1)
    def _():
        t = tgt_ref[:, 0, :]
        t = jnp.concatenate([t[0:1], t[1:2], t[2:3], jnp.zeros((1, 80), F32)], axis=1)
        t = pltpu.roll(jnp.broadcast_to(t, (8, 128)), lax.rem(me_ref[0], 8) * OWN, 1)[0:1]
        rows = []
        for c in range(4):
            v = color[c + 1 : c + 2] if c < 3 else -before[...]
            rows += [v[:, 128 * q : 128 * q + 128] for q in range(4)]
        rows.append(t)
        value = jnp.concatenate(rows, axis=0)
        for s in range(32):
            send_ref[s * ROWS : (s + 1) * ROWS] = value


def full(shape):
    return pl.BlockSpec(shape, lambda i, n=len(shape): (0,) * n)


def smem():
    return pl.BlockSpec(memory_space=pltpu.SMEM)


def slots(rows):
    return pl.BlockSpec((SPB, rows, RAYS), lambda i: (i, 0, 0))


def forward(me, geo, entry, counts, tgt, w_in, w_mid, w_out, b_hid, b_out, freqs, delta):
    res = [jax.ShapeDtypeStruct((32 * ROWS, 128), F32), jax.ShapeDtypeStruct((SAMP, 8, RAYS), F32)]
    res += [jax.ShapeDtypeStruct((SAMP, H, RAYS), BF16)] * 8 + [jax.ShapeDtypeStruct((SAMP, H, RAYS), F32)] * 3
    return pl.pallas_call(
        lambda *refs: forward_kernel(*refs, delta=delta),
        grid=(STEPS,),
        in_specs=[smem()] + [full(x.shape) for x in (geo, entry, counts, tgt, w_in, w_mid, w_out, b_hid, b_out, freqs)],
        out_specs=[full((32 * ROWS, 128)), slots(8)] + [slots(H)] * 11,
        out_shape=res,
        scratch_shapes=[
            pltpu.VMEM((3, H, H), BF16), pltpu.VMEM((3, H, H), BF16), pltpu.VMEM((16, H), BF16),
            pltpu.VMEM((3, H, 128), F32), pltpu.VMEM((H, RAYS), F32), pltpu.VMEM((H, RAYS), F32),
            pltpu.VMEM((1, RAYS), F32), pltpu.VMEM((8, RAYS), F32),
        ],
        compiler_params=pltpu.CompilerParams(vmem_limit_bytes=60 * 1024 * 1024),
        name="fwd",
    )(me, geo, entry, counts, tgt, w_in, w_mid, w_out, b_hid, b_out, freqs)


def backward_kernel(
    me_ref, recv_ref, counts_ref, win_ref, wmid_ref, wout_ref, out_ref,
    fh_ref, fl_ref, h1h_ref, h1l_ref, h2h_ref, h2l_ref, h3h_ref, h3l_ref, s1_ref, s2_ref, s3_ref,
    pix_ref, mine_ref, other_ref,
    wh, wl, woT, g_all, adj, pixs, acc, bacc, gacc, goacc,
    *, delta, factor,
):
    step = pl.program_id(0)

    @pl.when(step == 0)
    def _():
        me = me_ref[0]
        for i in range(2):
            wh[i], wl[i] = split(wmid_ref[0, i])
        w8 = jnp.concatenate([wout_ref[0], jnp.zeros((4, H), F32)], axis=0)
        hi, lo = split(w8)
        hi, lo = hi.astype(F32), lo.astype(F32)
        woT[...] = jnp.concatenate([hi, hi, lo, jnp.zeros((104, H), F32)], axis=0).T.astype(BF16)
        acc[...] = jnp.zeros_like(acc)
        bacc[...] = jnp.zeros_like(bacc)
        gacc[...] = jnp.zeros_like(gacc)
        goacc[...] = jnp.zeros_like(goacc)
        zero = jnp.zeros((4, 128), F32)
        depth, own, pix, after = zero, zero, [zero] * 3, [zero] * 3
        for s in range(32):
            shade = jnp.exp(depth)
            own = jnp.where(me == s, shade, own)
            late = jnp.where(s > me, F32(1.0), F32(0.0))
            for c in range(3):
                part = shade * recv_ref[s * ROWS + 4 * c : s * ROWS + 4 * c + 4]
                pix[c] = pix[c] + part
                after[c] = after[c] + late * part
            depth = depth + recv_ref[s * ROWS + 12 : s * ROWS + 16]
        through = jnp.exp(depth)
        lane = lax.broadcasted_iota(jnp.int32, (8, 128), 1)
        sub = lax.broadcasted_iota(jnp.int32, (8, 128), 0)
        adj[...] = jnp.zeros_like(adj)
        log_adj = zero
        for c in range(3):
            rows = []
            for q in range(4):
                t = jnp.concatenate(
                    [recv_ref[(8 * q + s) * ROWS + 16 : (8 * q + s) * ROWS + 17] for s in range(8)], axis=0
                )
                if c:
                    t = pltpu.roll(t, 128 - OWN * c, 1)
                t = jnp.where(lax.div(lane, OWN) == sub, t, F32(0.0))
                rows.append(jnp.sum(t, axis=0, keepdims=True))
            target = jnp.concatenate(rows, axis=0)
            pixel = pix[c] + through
            pixs[4 * c : 4 * c + 4] = pixel
            dpix = F32(2.0 * factor) * (pixel - target)
            log_adj = log_adj + dpix * (after[c] + through)
            a = own * dpix
            for q in range(4):
                adj[c + 1 : c + 2, 128 * q : 128 * q + 128] = a[q : q + 1]
        for c in range(3):
            row = pixs[pl.ds(4 * c + lax.div(me, 8), 1), :]
            row = pltpu.roll(jnp.broadcast_to(row, (8, 128)), lax.rem(128 - lax.rem(me, 8) * OWN, 128), 1)
            pix_ref[c] = row[0:1, 0:OWN]
        log_adj = jnp.concatenate([log_adj[q : q + 1] for q in range(4)], axis=1)
        a8 = adj[...]
        counts = counts_ref[0]
        bef = jnp.zeros((1, RAYS), F32)
        ends, weights = [], []
        for j in range(SAMP):
            dep = jnp.where(j < counts, softplus(out_ref[j, 0:1]) * F32(delta), F32(0.0))
            weights.append(jnp.exp(-bef) * (F32(1.0) - jnp.exp(-dep)))
            bef = bef + dep
            ends.append(jnp.exp(-bef))
        later = jnp.zeros((8, RAYS), F32)
        first = lax.broadcasted_iota(jnp.int32, (8, RAYS), 0) == 0
        for j in reversed(range(SAMP)):
            sg = sigmoid(out_ref[j])
            ddep = jnp.sum(a8 * (ends[j] * sg - later), axis=0, keepdims=True) - log_adj
            ddep = jnp.where(j < counts, F32(delta) * ddep, F32(0.0))
            g = jnp.where(first, ddep * sg, a8 * weights[j] * (sg * (F32(1.0) - sg)))
            later = later + weights[j] * sg
            g_all[j] = g

    for j in range(SPB):
        g = g_all[step * SPB + j]
        gacc[...] += g[:, 0:128] + g[:, 128:256] + g[:, 256:384] + g[:, 384:512]
        gh, gl = split(g)
        ghf, glf = gh.astype(F32), gl.astype(F32)
        g16 = jnp.concatenate([ghf, glf], axis=0).astype(BF16)
        d1 = mm_nt(g16, h3h_ref[j])
        d2 = mm_nt(g16, h3l_ref[j])
        goacc[...] += d1[0:8] + d1[8:16] + d2[0:8] + d2[8:16]
        gk = jnp.concatenate([ghf, glf, ghf, jnp.zeros((104, RAYS), F32)], axis=0).astype(BF16)
        dh = mm(woT[...], gk)
        for i, (sg, hh, hl) in enumerate(((s3_ref, h2h_ref, h2l_ref), (s2_ref, h1h_ref, h1l_ref), (s1_ref, fh_ref, fl_ref))):
            dx = dh * sg[j]
            bacc[2 - i] += dx[:, 0:128] + dx[:, 128:256] + dx[:, 256:384] + dx[:, 384:512]
            xh, xl = split(dx)
            acc[2 - i] += mm_nt(hh[j], xh) + mm_nt(hh[j], xl) + mm_nt(hl[j], xh)
            if i < 2:
                dh = mm(wh[1 - i], xh) + mm(wh[1 - i], xl) + mm(wl[1 - i], xh)

    @pl.when(step == STEPS - 1)
    def _():
        core, chip = me_ref[1], me_ref[2]
        for k in range(4):
            q = lax.rem(chip + k, 4)
            for i in range(3):
                rows = pl.ds(96 * k + 32 * i, 32)
                mine_ref[rows] = acc[i, pl.ds((core * 4 + q) * 32, 32), :]
                other_ref[rows] = acc[i, pl.ds(((1 - core) * 4 + q) * 32, 32), :]
        lane = lax.broadcasted_iota(jnp.int32, (8, 128), 1)
        sub = lax.broadcasted_iota(jnp.int32, (8, 128), 0)
        hid = [jnp.sum(bacc[i].T, axis=0, keepdims=True) for i in range(3)]
        gb = jnp.broadcast_to(jnp.sum(gacc[...], axis=1, keepdims=True), (8, 128))
        gb = jnp.sum(jnp.where(lane == sub, gb, F32(0.0)), axis=0, keepdims=True)
        gb = jnp.concatenate([gb, jnp.zeros((1, 128), F32)], axis=1)
        small = jnp.concatenate([goacc[0:4]] + hid + [gb], axis=0)
        mine_ref[384:392] = small
        other_ref[384:392] = small


def backward(ids, recv, counts, w_in, w_mid, w_out, out, residuals, delta, factor):
    half = jax.ShapeDtypeStruct((392, H), F32)
    return pl.pallas_call(
        lambda *refs: backward_kernel(*refs, delta=delta, factor=factor),
        grid=(STEPS,),
        in_specs=[smem()] + [full(x.shape) for x in (recv, counts, w_in, w_mid, w_out, out)] + [slots(H)] * 11,
        out_specs=[full((3, 1, OWN)), full((392, H)), full((392, H))],
        out_shape=[jax.ShapeDtypeStruct((3, 1, OWN), F32), half, half],
        scratch_shapes=[
            pltpu.VMEM((2, H, H), BF16), pltpu.VMEM((2, H, H), BF16), pltpu.VMEM((H, 128), BF16),
            pltpu.VMEM((SAMP, 8, RAYS), F32), pltpu.VMEM((8, RAYS), F32), pltpu.VMEM((16, 128), F32),
            pltpu.VMEM((3, H, H), F32), pltpu.VMEM((3, H, 128), F32), pltpu.VMEM((8, 128), F32), pltpu.VMEM((8, H), F32),
        ],
        compiler_params=pltpu.CompilerParams(vmem_limit_bytes=60 * 1024 * 1024),
        name="bwd",
    )(ids, recv, counts, w_in, w_mid, w_out, out, *residuals)


def place_kernel(ids_ref, *refs):
    own, sib, (gin, gmid) = refs[0:4], refs[4], refs[5:]
    core, chip = ids_ref[1], ids_ref[2]
    for k in range(4):
        q = lax.rem(chip + 4 - k, 4)
        for side in range(2):
            src, base = (own[k], 0) if side == 0 else (sib, 96 * k)
            rows = pl.ds(((core if side == 0 else 1 - core) * 4 + q) * 32, 32)
            gin[0, rows] = src[base : base + 32]
            gmid[0, 0, rows] = src[base + 32 : base + 64]
            gmid[0, 1, rows] = src[base + 64 : base + 96]


def place(ids, own, sib):
    vm = pl.BlockSpec(memory_space=pltpu.VMEM)
    return pl.pallas_call(
        place_kernel,
        in_specs=[smem()] + [vm] * 5,
        out_specs=[vm, vm],
        out_shape=[jax.ShapeDtypeStruct((1, H, H), F32), jax.ShapeDtypeStruct((1, 2, H, H), F32)],
        name="place",
    )(ids, *own, sib)


def shards(geometry, entry, counts, targets, w_in, w_mid, w_out, b_hid, b_out, freqs):
    slabs = lax.axis_size("slab")
    delta = 3.0 / (SAMP * slabs)
    factor = 1.0 / math.sqrt(3.0 * lax.axis_size("rays") * slabs * OWN)
    me = lax.axis_index("slab")
    ray = lax.axis_index("rays")
    ids = jnp.stack([me, lax.rem(ray, 2), lax.div(ray, 2)]).astype(jnp.int32)
    send, out, *residuals = forward(
        ids, geometry, entry, counts, targets, w_in, w_mid, w_out, b_hid, b_out, freqs, delta
    )
    recv = lax.all_to_all(send.reshape(32, 1, ROWS * 128), "slab", 0, 0, tiled=True).reshape(32 * ROWS, 128)
    pixels, mine, other = backward(ids, recv, counts, w_in, w_mid, w_out, out, residuals, delta, factor)
    swap = [(i, i ^ 1) for i in range(8)]
    along = [[(i, (i + 2 * k) % 8) for i in range(8)] for k in range(4)]
    total = mine + lax.ppermute(other, "rays", swap)
    small = total[384:392]
    parts = [jnp.concatenate([total[96 * k : 96 * k + 96], small], axis=0) for k in range(4)]
    got = [lax.ppermute(parts[k], "rays", along[k]) for k in range(1, 4)]
    done = parts[0] + got[0] + got[1] + got[2]
    chunk = done[0:96]
    own = [chunk] + [lax.ppermute(chunk, "rays", along[k]) for k in range(1, 4)]
    sib = lax.ppermute(jnp.concatenate(own, axis=0), "rays", swap)
    grad_in, grad_mid = place(ids, own, sib)
    small = done[96:104]
    return pixels, grad_in, grad_mid, small[None, 0:4], small[None, 4:7], small[7:8, 0:4]


def solution(mesh):
    in_specs = (
        P(None, "rays", None),
        P("slab", "rays", None),
        P("slab", "rays", None),
        P(None, "rays", "slab"),
        P("slab", None, None),
        P("slab", None, None, None),
        P("slab", None, None),
        P("slab", None, None),
        P("slab", None),
        P("slab", None, None),
    )
    out_specs = (
        P(None, "rays", "slab"),
        P("slab", None, None),
        P("slab", None, None, None),
        P("slab", None, None),
        P("slab", None, None),
        P("slab", None),
    )
    return jax.shard_map(shards, mesh=mesh, in_specs=in_specs, out_specs=out_specs, check_vma=False)
```

profile of v0, /device:TPU:1, one launch (start us, length us, event | category | flops | bytes accessed | tf_op | source)
XLA Modules:
  0.0 95.1 jit_solution(2393340718932581802)
XLA Ops:
  0.6 1.3 %copy.20.refs_10_ = f32[1,3,128]{2,1,0:T(4,128)} copy(f32[1,3,128]{2,0,1:T(1,128)} %param.19) | data formatting | bytes 3072 | tf_op args[9]
  1.9 1.3 %copy.19.refs_8_ = f32[1,3,256]{2,1,0:T(4,128)} copy(f32[1,3,256]{2,0,1:T(1,128)} %param.17) | data formatting | bytes 6144 | tf_op args[7]
  3.2 0.7 pad_add_fusion.refs_0_.ids_ref
  3.8 19.0 %fwd.1 = (f32[544,128]{1,0:T(8,128)}, f32[8,8,512]{2,1,0:T(8,128)}, bf16[8,256,512]{2,1,0:T(8,128)(2,1)}, bf16[8,256,512]{2,1,0:T(8,128)(2,1)}, bf16[8,256,512]{...) custom-call(s32[3]{0:T(128)} %pad_add_fusion.refs_0_.ids_ref, ...), custom_call_target="tpu_custom_call" | custom-call | tf_op jit(solution)/shard_map/fwd/pallas_call | solution.py:170
  22.9 23.9 %all_to_all.5 = f32[32,1,2176]{2,1,0:T(1,128)} all-to-all(f32[32,1,2176]{2,1,0:T(1,128)} %bitcast.10), channel_id=1, replica_groups=mesh['slab'=32,'rays'=8] {'slab'}, dimensions={0} | all-to-all | bytes 557056 | tf_op jit(solution)/shard_map/all_to_all | solution.py:357
  46.8 18.9 %bwd.1 = (f32[3,1,16]{2,1,0:T(1,128)}, f32[392,256]{1,0:T(8,128)}, f32[392,256]{1,0:T(8,128)}) custom-call(s32[3]{0:T(128)} %pad_add_fusion.refs_0_.ids_ref, f32[544,128]{1,0:T(8,128)} %bitcast.9, s32[1,1,512]{2,1,0:T(1,128)} %refs_2_.3, f32[1,256,256]{2,1,0:T(8,128)} %refs_3_.3, f32[1,2,256,256]{3,2,1,0:T(8,128)} %refs_4_.3, f32[1,4,256]{2,1,0:T(4,128)} %refs_5_.3, ...), custom_call_target="tpu_custom_call" | custom-call | tf_op jit(solution)/shard_map/bwd/pallas_call | solution.py:307
  65.7 2.2 %collective-permute-start = (f32[392,256]{1,0:T(8,128)}, f32[392,256]{1,0:T(8,128)S(1)}, u32[]{:S(2)}, u32[]{:S(2)}) collective-permute-start(f32[392,256]{1,0:T(8,128)} %get-tuple-element.39), channel_id=1, source_target_pairs={{0,1},{1,0},{2,3},{3,2},{4,5},{5,4},{6,7},{7,6},{8,9},{9,8},{10,11... | collective-permute-start | bytes 1204232 | tf_op jit(solution)/shard_map/ppermute | solution.py:361
  68.0 1.6 %collective-permute-done = f32[392,256]{1,0:T(8,128)S(1)} collective-permute-done((f32[392,256]{1,0:T(8,128)}, f32[392,256]{1,0:T(8,128)S(1)}, u32[]{:S(2)}, u32[]{:S(2)}) %collective-permute-start) | collective-permute-done | bytes 401440 | tf_op jit(solution)/shard_map/ppermute | solution.py:361
  69.5 1.1 %add.12 = f32[392,256]{1,0:T(8,128)S(1)} add(f32[392,256]{1,0:T(8,128)} %get-tuple-element.38, f32[392,256]{1,0:T(8,128)S(1)} %collective-permute-done) | non-fusion elementwise | flops 100352 | bytes 1204224 | tf_op jit(solution)/shard_map/add | solution.py:361
  70.7 2.6 %collective-permute-start.3 = (f32[104,256]{1,0:T(8,128)S(1)}, f32[104,256]{1,0:T(8,128)S(1)}, u32[]{:S(2)}, u32[]{:S(2)}) collective-permute-start(f32[104,256]{1,0:T(8,128)S(1)} %concatenate.20), channel_id=1, source_target_pairs={{0,6},{1,7},{2,0},{3,1},{4,2},{5,3},{6,4},{7,5},{8,14},{9,15},{10,... | collective-permute-start | bytes 319496 | tf_op jit(solution)/shard_map/ppermute | solution.py:364
  73.2 0.1 collective-permute-start.1
  73.3 1.7 %collective-permute-start.2 = (f32[104,256]{1,0:T(8,128)S(1)}, f32[104,256]{1,0:T(8,128)S(1)}, u32[]{:S(2)}, u32[]{:S(2)}) collective-permute-start(f32[104,256]{1,0:T(8,128)S(1)} %get-tuple-element.58), channel_id=1, source_target_pairs={{0,4},{1,5},{2,6},{3,7},{4,0},{5,1},{6,2},{7,3},{8,12},{9,13},{10,... | collective-permute-start | bytes 319496 | tf_op jit(solution)/shard_map/ppermute | solution.py:364
  75.0 0.1 collective-permute-done.3
  75.2 5.9 %collective-permute-done.1 = f32[104,256]{1,0:T(8,128)S(1)} collective-permute-done((f32[104,256]{1,0:T(8,128)S(1)}, f32[104,256]{1,0:T(8,128)S(1)}, u32[]{:S(2)}, u32[]{:S(2)}) %collective-permute-start.1) | collective-permute-done | bytes 106528 | tf_op jit(solution)/shard_map/ppermute | solution.py:364
  81.0 0.0 collective-permute-done.2
  81.1 0.0 copy-start
  81.1 0.1 collective-permute-start.6
  81.2 0.3 collective-permute-start.5
  81.5 1.2 %collective-permute-start.4 = (f32[96,256]{1,0:T(8,128)S(1)}, f32[96,256]{1,0:T(8,128)S(1)}, u32[]{:S(2)}, u32[]{:S(2)}) collective-permute-start(f32[96,256]{1,0:T(8,128)S(1)} %slice.42.refs_0_), channel_id=1, source_target_pairs={{0,2},{1,3},{2,4},{3,5},{4,6},{5,7},{6,0},{7,1},{8,10},{9,11},{10,... | collective-permute-start | bytes 294920 | tf_op jit(solution)/shard_map/ppermute | solution.py:367
  82.6 0.5 slice.45
  83.2 1.5 %collective-permute-done.6.refs_3_ = f32[96,256]{1,0:T(8,128)S(1)} collective-permute-done((f32[96,256]{1,0:T(8,128)S(1)}, f32[96,256]{1,0:T(8,128)S(1)}, u32[]{:S(2)}, u32[]{:S(2)}) %collective-permute-start.6) | collective-permute-done | bytes 98336 | tf_op jit(solution)/shard_map/ppermute | solution.py:367
  84.6 1.6 %collective-permute-done.5.refs_2_ = f32[96,256]{1,0:T(8,128)S(1)} collective-permute-done((f32[96,256]{1,0:T(8,128)S(1)}, f32[96,256]{1,0:T(8,128)S(1)}, u32[]{:S(2)}, u32[]{:S(2)}) %collective-permute-start.5) | collective-permute-done | bytes 98336 | tf_op jit(solution)/shard_map/ppermute | solution.py:367
  86.3 1.0 %collective-permute-done.4.refs_1_ = f32[96,256]{1,0:T(8,128)S(1)} collective-permute-done((f32[96,256]{1,0:T(8,128)S(1)}, f32[96,256]{1,0:T(8,128)S(1)}, u32[]{:S(2)}, u32[]{:S(2)}) %collective-permute-start.4) | collective-permute-done | bytes 98336 | tf_op jit(solution)/shard_map/ppermute | solution.py:367
  87.3 3.5 %collective-permute-start.7 = (f32[384,256]{1,0:T(8,128)S(1)}, f32[384,256]{1,0:T(8,128)S(1)}, u32[]{:S(2)}, u32[]{:S(2)}) collective-permute-start(f32[384,256]{1,0:T(8,128)S(1)} %pad_maximum_fusion), channel_id=1, source_target_pairs={{0,1},{1,0},{2,3},{3,2},{4,5},{5,4},{6,7},{7,6},{8,9},{9,8},{10,11... | collective-permute-start | bytes 1179656 | tf_op jit(solution)/shard_map/ppermute | solution.py:368
  90.8 0.6 copy.22
  91.4 0.6 slice_bitcast_fusion.1
  92.0 0.2 collective-permute-done.7.refs_4_
  92.1 0.0 copy-done
  92.1 0.0 copy-done.2
  92.2 0.0 copy-done.3
  92.2 0.7 copy-done.1
  92.9 2.1 %place.1 = (f32[1,256,256]{2,1,0:T(8,128)}, f32[1,2,256,256]{3,2,1,0:T(8,128)}) custom-call(s32[3]{0:T(128)} %pad_add_fusion.refs_0_.ids_ref, f32[96,256]{1,0:T(8,128)} %copy-done, f32[96,256]{1,0:T(8,128)} %copy-done.4, f32[96,256]{1,0:T(8,128)} %copy-done.3, f32[96,256]{1,0:T(8,128)} %copy-done.2, f32[384,256]{1,0:T(8,128)} %copy-done.1), custom_call_target="tpu_custom_call" | custom-call | tf_op jit(solution)/shard_map/place/pallas_call | solution.py:338
  (13 shorter events, 0.1 us)
Async XLA Ops:
  65.7 3.8 %collective-permute-start = (f32[392,256]{1,0:T(8,128)}, f32[392,256]{1,0:T(8,128)S(1)}, u32[]{:S(2)}, u32[]{:S(2)}) collective-permute-start(f32[392,256]{1,0:T(8,128)} %get-tuple-element.39), channel_id=1, source_target_pairs={{0,1},{1,0},{2,3},{3,2},{4,5},{5,4},{6,7},{7,6},{8,9},{9,8},{10,11... | collective-permute-start | bytes 1204232 | tf_op jit(solution)/shard_map/ppermute | solution.py:361
  70.7 4.5 %collective-permute-start.3 = (f32[104,256]{1,0:T(8,128)S(1)}, f32[104,256]{1,0:T(8,128)S(1)}, u32[]{:S(2)}, u32[]{:S(2)}) collective-permute-start(f32[104,256]{1,0:T(8,128)S(1)} %concatenate.20), channel_id=1, source_target_pairs={{0,6},{1,7},{2,0},{3,1},{4,2},{5,3},{6,4},{7,5},{8,14},{9,15},{10,... | collective-permute-start | bytes 319496 | tf_op jit(solution)/shard_map/ppermute | solution.py:364
  73.2 7.8 %collective-permute-start.1 = (f32[104,256]{1,0:T(8,128)S(1)}, f32[104,256]{1,0:T(8,128)S(1)}, u32[]{:S(2)}, u32[]{:S(2)}) collective-permute-start(f32[104,256]{1,0:T(8,128)S(1)} %get-tuple-element.57), channel_id=1, source_target_pairs={{0,2},{1,3},{2,4},{3,5},{4,6},{5,7},{6,0},{7,1},{8,10},{9,11},{10,... | collective-permute-start | bytes 319496 | tf_op jit(solution)/shard_map/ppermute | solution.py:364
  73.3 7.7 %collective-permute-start.2 = (f32[104,256]{1,0:T(8,128)S(1)}, f32[104,256]{1,0:T(8,128)S(1)}, u32[]{:S(2)}, u32[]{:S(2)}) collective-permute-start(f32[104,256]{1,0:T(8,128)S(1)} %get-tuple-element.58), channel_id=1, source_target_pairs={{0,4},{1,5},{2,6},{3,7},{4,0},{5,1},{6,2},{7,3},{8,12},{9,13},{10,... | collective-permute-start | bytes 319496 | tf_op jit(solution)/shard_map/ppermute | solution.py:364
  81.1 11.1 %copy-start = (f32[96,256]{1,0:T(8,128)}, f32[96,256]{1,0:T(8,128)S(1)}, u32[]{:S(2)}) copy-start(f32[96,256]{1,0:T(8,128)S(1)} %slice.42.refs_0_) | copy-start | bytes 294916
  81.1 3.5 %collective-permute-start.6 = (f32[96,256]{1,0:T(8,128)S(1)}, f32[96,256]{1,0:T(8,128)S(1)}, u32[]{:S(2)}, u32[]{:S(2)}) collective-permute-start(f32[96,256]{1,0:T(8,128)S(1)} %slice.42.refs_0_), channel_id=1, source_target_pairs={{0,6},{1,7},{2,0},{3,1},{4,2},{5,3},{6,4},{7,5},{8,14},{9,15},{10,... | collective-permute-start | bytes 294920 | tf_op jit(solution)/shard_map/ppermute | solution.py:367
  81.2 5.1 %collective-permute-start.5 = (f32[96,256]{1,0:T(8,128)S(1)}, f32[96,256]{1,0:T(8,128)S(1)}, u32[]{:S(2)}, u32[]{:S(2)}) collective-permute-start(f32[96,256]{1,0:T(8,128)S(1)} %slice.42.refs_0_), channel_id=1, source_target_pairs={{0,4},{1,5},{2,6},{3,7},{4,0},{5,1},{6,2},{7,3},{8,12},{9,13},{10,... | collective-permute-start | bytes 294920 | tf_op jit(solution)/shard_map/ppermute | solution.py:367
  81.5 5.8 %collective-permute-start.4 = (f32[96,256]{1,0:T(8,128)S(1)}, f32[96,256]{1,0:T(8,128)S(1)}, u32[]{:S(2)}, u32[]{:S(2)}) collective-permute-start(f32[96,256]{1,0:T(8,128)S(1)} %slice.42.refs_0_), channel_id=1, source_target_pairs={{0,2},{1,3},{2,4},{3,5},{4,6},{5,7},{6,0},{7,1},{8,10},{9,11},{10,... | collective-permute-start | bytes 294920 | tf_op jit(solution)/shard_map/ppermute | solution.py:367
  84.6 7.5 %copy-start.2 = (f32[96,256]{1,0:T(8,128)}, f32[96,256]{1,0:T(8,128)S(1)}, u32[]{:S(2)}) copy-start(f32[96,256]{1,0:T(8,128)S(1)} %collective-permute-done.6.refs_3_) | copy-start | bytes 294916
  86.3 5.9 %copy-start.3 = (f32[96,256]{1,0:T(8,128)}, f32[96,256]{1,0:T(8,128)S(1)}, u32[]{:S(2)}) copy-start(f32[96,256]{1,0:T(8,128)S(1)} %collective-permute-done.5.refs_2_) | copy-start | bytes 294916
  87.3 4.9 %copy-start.4 = (f32[96,256]{1,0:T(8,128)}, f32[96,256]{1,0:T(8,128)S(1)}, u32[]{:S(2)}) copy-start(f32[96,256]{1,0:T(8,128)S(1)} %collective-permute-done.4.refs_1_) | copy-start | bytes 294916
  87.3 4.8 %collective-permute-start.7 = (f32[384,256]{1,0:T(8,128)S(1)}, f32[384,256]{1,0:T(8,128)S(1)}, u32[]{:S(2)}, u32[]{:S(2)}) collective-permute-start(f32[384,256]{1,0:T(8,128)S(1)} %pad_maximum_fusion), channel_id=1, source_target_pairs={{0,1},{1,0},{2,3},{3,2},{4,5},{5,4},{6,7},{7,6},{8,9},{9,8},{10,11... | collective-permute-start | bytes 1179656 | tf_op jit(solution)/shard_map/ppermute | solution.py:368
  92.2 0.8 copy-start.1
where the time goes:
time: 95.3 us; the launch traced here: 95.1 us
  Pallas kernels  40.1 us (42%)
  blocking collectives  23.9 us (25%)
  waiting for transfers between devices  11.9 us (12%)
  starting transfers between devices  11.6 us (12%)
  local copies, waits for them, and re-layouts  5.03 us (5%)
  other arithmetic  1.79 us (2%)
    all_to_all x1, blocking collectives, shards(): lax.all_to_all(send.reshape(32, 1, ROWS * 128), 'slab', 0, 0, tiled=True)  23.9 us
    pallas_call x1, Pallas kernels, forward(): pl.pallas_call(lambda *refs: forward_kernel(*refs, delta=delta), grid=(ST...  19 us
    pallas_call x1, Pallas kernels, backward(): pl.pallas_call(lambda *refs: backward_kernel(*refs, delta=delta, factor=f...  18.9 us
    ppermute x3, waiting for transfers between devices, shards(): got = [lax.ppermute(parts[k], 'rays', along[k]) for k in range(1, 4)]  5.99 us
    ppermute x3, starting transfers between devices, shards(): got = [lax.ppermute(parts[k], 'rays', along[k]) for k in range(1, 4)]  4.36 us
    ppermute x3, waiting for transfers between devices, shards(): own = [chunk] + [lax.ppermute(chunk, 'rays', along[k]) for k in range(1, 4)]  4.14 us
    unnamed x13, local copies, waits for them, and re-layouts  3.88 us
    ppermute x1, starting transfers between devices, shards(): sib = lax.ppermute(jnp.concatenate(own, axis=0), 'rays', swap)  3.46 us
  transfers between devices with their start and end apart: 8, of which 7 were waited for; matrix products, arithmetic and copies ran while one was open for 2% of the time, Pallas kernels for 0%

commit v1 on v0

--- a/solution.py
+++ b/solution.py
@@ -16,6 +16,8 @@
 SPB = 2
 STEPS = SAMP // SPB
 F32 = jnp.float32
+LOG2E = 1.4426950408889634
+LN2 = 0.6931471805599453
 BF16 = jnp.bfloat16
 NT = (((1,), (1,)), ((), ()))
 
@@ -58,19 +60,21 @@
     return jnp.maximum(x, F32(0.0)) + (jnp.log(w) + (u - (w - F32(1.0))))
 
 
+def softplus2(x):
+    v = jnp.exp2(jnp.minimum(x, F32(100.0)))
+    log = lax.log2(F32(1.0 - 2.0**-23) + v)
+    return jnp.maximum(jnp.maximum(log, v * (F32(LOG2E) - F32(0.5 * LOG2E) * v)), x)
+
+
 def sigmoid(x):
     u = jnp.exp(-jnp.abs(x))
     return jnp.where(x >= 0, F32(1.0), u) / (F32(1.0) + u)
 
 
-def column(row):
-    return jnp.broadcast_to(row, (8, row.shape[1])).T[:, 0:1]
-
-
 def forward_kernel(
     me_ref, geo_ref, entry_ref, counts_ref, tgt_ref, win_ref, wmid_ref, wout_ref, bhid_ref, bout_ref, freqs_ref,
     send_ref, out_ref, fh_ref, fl_ref, h1h_ref, h1l_ref, h2h_ref, h2l_ref, h3h_ref, h3l_ref, s1_ref, s2_ref, s3_ref,
-    wh, wl, wo, bias, rot, feat, before, color,
+    wcat, wo, bias, rot, feat, before, color,
     *, delta,
 ):
     step = pl.program_id(0)
@@ -78,15 +82,16 @@
     @pl.when(step == 0)
     def _():
         for i in range(3):
-            w = win_ref[0] if i == 0 else wmid_ref[0, i - 1]
+            w = win_ref[0] * F32(LOG2E) if i == 0 else wmid_ref[0, i - 1]
             hi, lo = split(w.T)
-            wh[i] = hi
-            wl[i] = lo
-            bias[i] = jnp.broadcast_to(column(bhid_ref[0, i : i + 1, :]), (H, 128))
-        w8 = jnp.concatenate([wout_ref[0], jnp.zeros((4, H), F32)], axis=0)
+            wcat[i, :, 0:256] = hi
+            wcat[i, :, 256:512] = hi
+            wcat[i, :, 512:768] = lo
+            bias[i] = jnp.broadcast_to(bhid_ref[i] * F32(LOG2E), (128, H)).T
+        w8 = jnp.concatenate([wout_ref[0] * F32(LN2), jnp.zeros((4, H), F32)], axis=0)
         hi, lo = split(w8)
         wo[...] = jnp.concatenate([hi.astype(F32), lo.astype(F32)], axis=0).astype(BF16)
-        ft = jnp.concatenate([freqs_ref[0], jnp.zeros((5, FE), F32)], axis=0).T
+        ft = jnp.concatenate([freqs_ref[0], freqs_ref[1], freqs_ref[2], jnp.zeros((5, FE), F32)], axis=0).T
         geo = geo_ref[:, 0, :]
         a = ft[:, 0:1] * geo[0:1] + ft[:, 1:2] * geo[1:2] + ft[:, 2:3] * geo[2:3]
         d = ft[:, 0:1] * geo[3:4] + ft[:, 1:2] * geo[4:5] + ft[:, 2:3] * geo[5:6]
@@ -100,10 +105,12 @@
         before[...] = jnp.zeros_like(before)
         color[...] = jnp.zeros_like(color)
 
+    n = step * SPB
+
     def slot_input(j):
         s, c = feat[0:FE], feat[FE:]
-        fh_ref[j, 0:FE], fl_ref[j, 0:FE] = split(s)
-        fh_ref[j, FE:], fl_ref[j, FE:] = split(c)
+        fh_ref[n + j, 0:FE], fl_ref[n + j, 0:FE] = split(s)
+        fh_ref[n + j, FE:], fl_ref[n + j, FE:] = split(c)
         rs, rc = rot[0:FE], rot[FE:]
         feat[0:FE] = s * rc + c * rs
         feat[FE:] = c * rc - s * rs
@@ -114,22 +121,22 @@
     sigs = [s1_ref, s2_ref, s3_ref]
     parts = [(j, k) for j in range(SPB) for k in range(2)]
     for i in range(3):
-        b = bias[i, :, 0:1]
+        b = jnp.concatenate([bias[i], bias[i]], axis=1)
         for j, k in parts:
             lanes = slice(256 * k, 256 * k + 256)
-            hi = srcs[i][0][j, :, lanes]
-            lo = srcs[i][1][j, :, lanes]
-            x = mm(wh[i], hi) + mm(wh[i], lo) + mm(wl[i], hi) + b
-            h = softplus(x)
-            sigs[i][j, :, lanes] = jnp.exp(x - h)
-            srcs[i + 1][0][j, :, lanes], srcs[i + 1][1][j, :, lanes] = split(h)
+            hi = srcs[i][0][n + j, :, lanes]
+            lo = srcs[i][1][n + j, :, lanes]
+            x = mm(wcat[i], jnp.concatenate([hi, lo, hi], axis=0)) + b
+            h = softplus2(x)
+            sigs[i][n + j, :, lanes] = jnp.exp2(x - h)
+            srcs[i + 1][0][n + j, :, lanes], srcs[i + 1][1][n + j, :, lanes] = split(h)
     bo = jnp.concatenate([bout_ref[0:1, :], jnp.zeros((1, 124), F32)], axis=1)
     bo = jnp.broadcast_to(bo, (128, 128)).T[0:8, 0:1]
     for j in range(SPB):
-        d1 = mm(wo[...], h3h_ref[j])
-        d2 = mm(wo[...], h3l_ref[j])
+        d1 = mm(wo[...], h3h_ref[n + j])
+        d2 = mm(wo[...], h3l_ref[n + j])
         o = d1[0:8] + d1[8:16] + d2[0:8] + d2[8:16] + bo
-        out_ref[j] = o
+        out_ref[step * SPB + j] = o
         alive = step * SPB + j < counts_ref[0]
         depth = jnp.where(alive, softplus(o[0:1]) * F32(delta), F32(0.0))
         bef = before[...]
@@ -152,6 +159,14 @@
             send_ref[s * ROWS : (s + 1) * ROWS] = value
 
 
+def keep(x):
+    return pltpu.with_memory_space_constraint(x, pltpu.VMEM)
+
+
+def vmem():
+    return pl.BlockSpec(memory_space=pltpu.VMEM)
+
+
 def full(shape):
     return pl.BlockSpec(shape, lambda i, n=len(shape): (0,) * n)
 
@@ -160,25 +175,21 @@
     return pl.BlockSpec(memory_space=pltpu.SMEM)
 
 
-def slots(rows):
-    return pl.BlockSpec((SPB, rows, RAYS), lambda i: (i, 0, 0))
-
-
 def forward(me, geo, entry, counts, tgt, w_in, w_mid, w_out, b_hid, b_out, freqs, delta):
-    res = [jax.ShapeDtypeStruct((32 * ROWS, 128), F32), jax.ShapeDtypeStruct((SAMP, 8, RAYS), F32)]
-    res += [jax.ShapeDtypeStruct((SAMP, H, RAYS), BF16)] * 8 + [jax.ShapeDtypeStruct((SAMP, H, RAYS), F32)] * 3
+    res = [jax.ShapeDtypeStruct((32 * ROWS, 128), F32), pltpu.VMEM((SAMP, 8, RAYS), F32)]
+    res += [pltpu.VMEM((SAMP, H, RAYS), BF16)] * 8 + [pltpu.VMEM((SAMP, H, RAYS), F32)] * 3
     return pl.pallas_call(
         lambda *refs: forward_kernel(*refs, delta=delta),
         grid=(STEPS,),
         in_specs=[smem()] + [full(x.shape) for x in (geo, entry, counts, tgt, w_in, w_mid, w_out, b_hid, b_out, freqs)],
-        out_specs=[full((32 * ROWS, 128)), slots(8)] + [slots(H)] * 11,
+        out_specs=[full((32 * ROWS, 128)), vmem()] + [vmem()] * 11,
         out_shape=res,
         scratch_shapes=[
-            pltpu.VMEM((3, H, H), BF16), pltpu.VMEM((3, H, H), BF16), pltpu.VMEM((16, H), BF16),
+            pltpu.VMEM((3, H, 3 * H), BF16), pltpu.VMEM((16, H), BF16),
             pltpu.VMEM((3, H, 128), F32), pltpu.VMEM((H, RAYS), F32), pltpu.VMEM((H, RAYS), F32),
             pltpu.VMEM((1, RAYS), F32), pltpu.VMEM((8, RAYS), F32),
         ],
-        compiler_params=pltpu.CompilerParams(vmem_limit_bytes=60 * 1024 * 1024),
+        compiler_params=pltpu.CompilerParams(vmem_limit_bytes=28 * 1024 * 1024),
         name="fwd",
     )(me, geo, entry, counts, tgt, w_in, w_mid, w_out, b_hid, b_out, freqs)
 
@@ -187,7 +198,7 @@
     me_ref, recv_ref, counts_ref, win_ref, wmid_ref, wout_ref, out_ref,
     fh_ref, fl_ref, h1h_ref, h1l_ref, h2h_ref, h2l_ref, h3h_ref, h3l_ref, s1_ref, s2_ref, s3_ref,
     pix_ref, mine_ref, other_ref,
-    wh, wl, woT, g_all, adj, pixs, acc, bacc, gacc, goacc,
+    wcat, wo, g_all, adj, pixs, acc, bacc, gacc, goacc, dh_buf,
     *, delta, factor,
 ):
     step = pl.program_id(0)
@@ -196,11 +207,14 @@
     def _():
         me = me_ref[0]
         for i in range(2):
-            wh[i], wl[i] = split(wmid_ref[0, i])
+            hi, lo = split(wmid_ref[0, i])
+            wcat[i, :, 0:256] = hi
+            wcat[i, :, 256:512] = hi
+            wcat[i, :, 512:768] = lo
         w8 = jnp.concatenate([wout_ref[0], jnp.zeros((4, H), F32)], axis=0)
         hi, lo = split(w8)
         hi, lo = hi.astype(F32), lo.astype(F32)
-        woT[...] = jnp.concatenate([hi, hi, lo, jnp.zeros((104, H), F32)], axis=0).T.astype(BF16)
+        wo[...] = jnp.concatenate([hi, hi, lo, jnp.zeros((104, H), F32)], axis=0).T[:, 0:32].astype(BF16)
         acc[...] = jnp.zeros_like(acc)
         bacc[...] = jnp.zeros_like(bacc)
         gacc[...] = jnp.zeros_like(gacc)
@@ -263,24 +277,39 @@
             later = later + weights[j] * sg
             g_all[j] = g
 
+    n = step * SPB
     for j in range(SPB):
         g = g_all[step * SPB + j]
         gacc[...] += g[:, 0:128] + g[:, 128:256] + g[:, 256:384] + g[:, 384:512]
+        gb = [[jnp.broadcast_to(g[c : c + 1, 128 * t : 128 * t + 128], (8, 128)) for t in range(4)] for c in range(4)]
+        for r in range(0, H, 16):
+            rows = slice(r, r + 16)
+            parts = [None] * 4
+            for t in range(4):
+                lanes = slice(128 * t, 128 * t + 128)
+                h3 = h3h_ref[n + j, rows, lanes].astype(F32) + h3l_ref[n + j, rows, lanes].astype(F32)
+                for c in range(4):
+                    p = jnp.concatenate([h3[0:8] * gb[c][t], h3[8:16] * gb[c][t]], axis=0)
+                    parts[c] = p if parts[c] is None else parts[c] + p
+            for c in range(4):
+                goacc[c, rows] += parts[c]
         gh, gl = split(g)
-        ghf, glf = gh.astype(F32), gl.astype(F32)
-        g16 = jnp.concatenate([ghf, glf], axis=0).astype(BF16)
-        d1 = mm_nt(g16, h3h_ref[j])
-        d2 = mm_nt(g16, h3l_ref[j])
-        goacc[...] += d1[0:8] + d1[8:16] + d2[0:8] + d2[8:16]
-        gk = jnp.concatenate([ghf, glf, ghf, jnp.zeros((104, RAYS), F32)], axis=0).astype(BF16)
-        dh = mm(woT[...], gk)
-        for i, (sg, hh, hl) in enumerate(((s3_ref, h2h_ref, h2l_ref), (s2_ref, h1h_ref, h1l_ref), (s1_ref, fh_ref, fl_ref))):
-            dx = dh * sg[j]
+        gh, gl = gh.astype(F32), gl.astype(F32)
+        gk = jnp.concatenate([gh, gl, gh, jnp.zeros((8, RAYS), F32)], axis=0).astype(BF16)
+        dh_buf[j] = mm(wo[...], gk)
+    sigs = (s3_ref, s2_ref, s1_ref)
+    hs = ((h2h_ref, h2l_ref), (h1h_ref, h1l_ref), (fh_ref, fl_ref))
+    for i in range(3):
+        lhs, rhs = [], []
+        for j in range(SPB):
+            dx = dh_buf[j] * sigs[i][n + j]
             bacc[2 - i] += dx[:, 0:128] + dx[:, 128:256] + dx[:, 256:384] + dx[:, 384:512]
             xh, xl = split(dx)
-            acc[2 - i] += mm_nt(hh[j], xh) + mm_nt(hh[j], xl) + mm_nt(hl[j], xh)
+            lhs += [hs[i][0][n + j], hs[i][0][n + j], hs[i][1][n + j]]
+            rhs += [xh, xl, xh]
             if i < 2:
-                dh = mm(wh[1 - i], xh) + mm(wh[1 - i], xl) + mm(wl[1 - i], xh)
+                dh_buf[j] = mm(wcat[1 - i], jnp.concatenate([xh, xl, xh], axis=0))
+        acc[2 - i] += mm_nt(jnp.concatenate(lhs, axis=1), jnp.concatenate(rhs, axis=1))
 
     @pl.when(step == STEPS - 1)
     def _():
@@ -289,39 +318,44 @@
             q = lax.rem(chip + k, 4)
             for i in range(3):
                 rows = pl.ds(96 * k + 32 * i, 32)
-                mine_ref[rows] = acc[i, pl.ds((core * 4 + q) * 32, 32), :]
-                other_ref[rows] = acc[i, pl.ds(((1 - core) * 4 + q) * 32, 32), :]
+                unit = F32(LN2 if i else 1.0)
+                mine_ref[rows] = acc[i, pl.ds((core * 4 + q) * 32, 32), :] * unit
+                other_ref[rows] = acc[i, pl.ds(((1 - core) * 4 + q) * 32, 32), :] * unit
         lane = lax.broadcasted_iota(jnp.int32, (8, 128), 1)
         sub = lax.broadcasted_iota(jnp.int32, (8, 128), 0)
         hid = [jnp.sum(bacc[i].T, axis=0, keepdims=True) for i in range(3)]
         gb = jnp.broadcast_to(jnp.sum(gacc[...], axis=1, keepdims=True), (8, 128))
         gb = jnp.sum(jnp.where(lane == sub, gb, F32(0.0)), axis=0, keepdims=True)
         gb = jnp.concatenate([gb, jnp.zeros((1, 128), F32)], axis=1)
-        small = jnp.concatenate([goacc[0:4]] + hid + [gb], axis=0)
+        outw = [jnp.sum(goacc[c].T, axis=0, keepdims=True) * F32(LN2) for c in range(4)]
+        small = jnp.concatenate(outw + hid + [gb], axis=0)
         mine_ref[384:392] = small
         other_ref[384:392] = small
 
 
 def backward(ids, recv, counts, w_in, w_mid, w_out, out, residuals, delta, factor):
-    half = jax.ShapeDtypeStruct((392, H), F32)
+    half = pltpu.VMEM((392, H), F32)
+    recv, out = keep(recv), keep(out)
+    residuals = [keep(x) for x in residuals]
     return pl.pallas_call(
         lambda *refs: backward_kernel(*refs, delta=delta, factor=factor),
         grid=(STEPS,),
-        in_specs=[smem()] + [full(x.shape) for x in (recv, counts, w_in, w_mid, w_out, out)] + [slots(H)] * 11,
-        out_specs=[full((3, 1, OWN)), full((392, H)), full((392, H))],
+        in_specs=[smem(), vmem()] + [full(x.shape) for x in (counts, w_in, w_mid, w_out)] + [vmem()] + [vmem()] * 11,
+        out_specs=[full((3, 1, OWN)), vmem(), vmem()],
         out_shape=[jax.ShapeDtypeStruct((3, 1, OWN), F32), half, half],
         scratch_shapes=[
-            pltpu.VMEM((2, H, H), BF16), pltpu.VMEM((2, H, H), BF16), pltpu.VMEM((H, 128), BF16),
+            pltpu.VMEM((2, H, 3 * H), BF16), pltpu.VMEM((H, 32), BF16),
             pltpu.VMEM((SAMP, 8, RAYS), F32), pltpu.VMEM((8, RAYS), F32), pltpu.VMEM((16, 128), F32),
-            pltpu.VMEM((3, H, H), F32), pltpu.VMEM((3, H, 128), F32), pltpu.VMEM((8, 128), F32), pltpu.VMEM((8, H), F32),
+            pltpu.VMEM((3, H, H), F32), pltpu.VMEM((3, H, 128), F32), pltpu.VMEM((8, 128), F32), pltpu.VMEM((4, H, 128), F32),
+            pltpu.VMEM((SPB, H, RAYS), F32),
         ],
-        compiler_params=pltpu.CompilerParams(vmem_limit_bytes=60 * 1024 * 1024),
+        compiler_params=pltpu.CompilerParams(vmem_limit_bytes=28 * 1024 * 1024),
         name="bwd",
     )(ids, recv, counts, w_in, w_mid, w_out, out, *residuals)
 
 
-def place_kernel(ids_ref, *refs):
-    own, sib, (gin, gmid) = refs[0:4], refs[4], refs[5:]
+def place_kernel(ids_ref, done, own1, own2, own3, sib, gin, gmid, gout, ghid, gbout):
+    own = (done, own1, own2, own3)
     core, chip = ids_ref[1], ids_ref[2]
     for k in range(4):
         q = lax.rem(chip + 4 - k, 4)
@@ -331,17 +365,22 @@
             gin[0, rows] = src[base : base + 32]
             gmid[0, 0, rows] = src[base + 32 : base + 64]
             gmid[0, 1, rows] = src[base + 64 : base + 96]
-
-
-def place(ids, own, sib):
-    vm = pl.BlockSpec(memory_space=pltpu.VMEM)
+    gout[0] = done[96:100]
+    for i in range(3):
+        ghid[i] = done[100 + i : 101 + i]
+    gbout[...] = done[103:104, 0:4]
+
+
+def place(ids, done, own, sib):
+    shapes = [(1, H, H), (1, 2, H, H), (1, 4, H), (3, 1, H), (1, 4)]
     return pl.pallas_call(
         place_kernel,
-        in_specs=[smem()] + [vm] * 5,
-        out_specs=[vm, vm],
-        out_shape=[jax.ShapeDtypeStruct((1, H, H), F32), jax.ShapeDtypeStruct((1, 2, H, H), F32)],
+        in_specs=[smem()] + [vmem()] * 5,
+        out_specs=[vmem()] * 5,
+        out_shape=[jax.ShapeDtypeStruct(x, F32) for x in shapes],
+        compiler_params=pltpu.CompilerParams(vmem_limit_bytes=16 * 1024 * 1024),
         name="place",
-    )(ids, *own, sib)
+    )(ids, *[keep(x) for x in (done, *own, sib)])
 
 
 def shards(geometry, entry, counts, targets, w_in, w_mid, w_out, b_hid, b_out, freqs):
@@ -352,7 +391,8 @@
     ray = lax.axis_index("rays")
     ids = jnp.stack([me, lax.rem(ray, 2), lax.div(ray, 2)]).astype(jnp.int32)
     send, out, *residuals = forward(
-        ids, geometry, entry, counts, targets, w_in, w_mid, w_out, b_hid, b_out, freqs, delta
+        ids, geometry, entry, counts, targets, w_in, w_mid, w_out,
+        b_hid.transpose(1, 0, 2), b_out, freqs.transpose(1, 0, 2), delta
     )
     recv = lax.all_to_all(send.reshape(32, 1, ROWS * 128), "slab", 0, 0, tiled=True).reshape(32 * ROWS, 128)
     pixels, mine, other = backward(ids, recv, counts, w_in, w_mid, w_out, out, residuals, delta, factor)
@@ -364,11 +404,10 @@
     got = [lax.ppermute(parts[k], "rays", along[k]) for k in range(1, 4)]
     done = parts[0] + got[0] + got[1] + got[2]
     chunk = done[0:96]
-    own = [chunk] + [lax.ppermute(chunk, "rays", along[k]) for k in range(1, 4)]
-    sib = lax.ppermute(jnp.concatenate(own, axis=0), "rays", swap)
-    grad_in, grad_mid = place(ids, own, sib)
-    small = done[96:104]
-    return pixels, grad_in, grad_mid, small[None, 0:4], small[None, 4:7], small[7:8, 0:4]
+    own = [lax.ppermute(chunk, "rays", along[k]) for k in range(1, 4)]
+    sib = lax.ppermute(jnp.concatenate([chunk] + own, axis=0), "rays", swap)
+    grad_in, grad_mid, grad_out, grad_hid, grad_bout = place(ids, done, own, sib)
+    return pixels, grad_in, grad_mid, grad_out, grad_hid.transpose(1, 0, 2), grad_bout
 
 
 def solution(mesh):

time: 95.3 us -> 80.5 us (0.84)
  Pallas kernels: 40.1 us -> 30.1 us
  local copies, waits for them, and re-layouts: 5.03 us -> 0.05 us
  waiting for transfers between devices: 11.9 us -> 13.3 us
  other arithmetic: 1.79 us -> 0.72 us
    pallas_call x1, Pallas kernels: 18.9 us -> 13.6 us  [backward(): pl.pallas_call(lambda *refs: backward_kernel(*refs, delta=delta, factor=f...]
    pallas_call x1, Pallas kernels: 19 us -> 15 us  [forward(): pl.pallas_call(lambda *refs: forward_kernel(*refs, delta=delta), grid=(ST...]
    unnamed x13 -> x2, local copies, waits for them, and re-layouts: 3.88 us -> 0.01 us
    ppermute x4, waiting for transfers between devices: 4.3 us -> 6 us  [the longest x3 4.65 us: shards(): own = [lax.ppermute(chunk, 'rays', along[k]) for k in range(1, 4)]]
    add x1, other arithmetic: 1.05 us -> 0.05 us  [shards(): total = mine + lax.ppermute(other, 'rays', swap)]
  transfers between devices with their start and end apart: 8 -> 8, of which waited for: 7 -> 7; matrix products, arithmetic and copies ran while one was open for 2% -> 0% of each run, Pallas kernels for 0% -> 0%
where the time goes in v1:
time: 80.5 us; the launch traced here: 80.3 us
  Pallas kernels  30.1 us (37%)
  blocking collectives  23.8 us (30%)
  waiting for transfers between devices  13.3 us (17%)
  starting transfers between devices  11.5 us (14%)
    all_to_all x1, blocking collectives, shards(): lax.all_to_all(send.reshape(32, 1, ROWS * 128), 'slab', 0, 0, tiled=True)  23.8 us
    pallas_call x1, Pallas kernels, forward(): pl.pallas_call(lambda *refs: forward_kernel(*refs, delta=delta), grid=(ST...  15 us
    pallas_call x1, Pallas kernels, backward(): pl.pallas_call(lambda *refs: backward_kernel(*refs, delta=delta, factor=f...  13.6 us
    ppermute x3, waiting for transfers between devices, shards(): got = [lax.ppermute(parts[k], 'rays', along[k]) for k in range(1, 4)]  5.98 us
    ppermute x3, waiting for transfers between devices, shards(): own = [lax.ppermute(chunk, 'rays', along[k]) for k in range(1, 4)]  4.65 us
    ppermute x3, starting transfers between devices, shards(): got = [lax.ppermute(parts[k], 'rays', along[k]) for k in range(1, 4)]  4.37 us
    ppermute x1, starting transfers between devices, shards(): sib = lax.ppermute(jnp.concatenate([chunk] + own, axis=0), 'rays', swap)  3.46 us
    ppermute x1, starting transfers between devices, shards(): total = mine + lax.ppermute(other, 'rays', swap)  2.16 us
  transfers between devices with their start and end apart: 8, of which 7 were waited for; matrix products, arithmetic and copies ran while one was open for 0% of the time, Pallas kernels for 0%

profile of v1, /device:TPU:1, one launch (start us, length us, event | category | flops | bytes accessed | tf_op | source)
XLA Modules:
  0.0 80.3 jit_solution(6991538178310162767)
XLA Ops:
  0.6 0.6 pad_add_fusion.refs_0_.ids_ref
  1.2 15.0 %fwd.1 = (f32[544,128]{1,0:T(8,128)}, f32[8,8,512]{2,1,0:T(8,128)S(1)}, bf16[8,256,512]{2,1,0:T(8,128)(2,1)S(1)}, bf16[8,256,512]{2,1,0:T(8,128)(2,1)S(1)}, bf16...) custom-call(s32[3]{0:T(128)} %pad_add_fusion.refs_0_.ids_ref, ...), custom_call_target="tpu_custom_call" | custom-call | tf_op jit(solution)/shard_map/fwd/pallas_call | solution.py:181
  16.3 23.8 %all_to_all.5 = f32[32,1,2176]{2,1,0:T(1,128)S(1)} all-to-all(f32[32,1,2176]{2,1,0:T(1,128)} %bitcast.9), channel_id=1, replica_groups=mesh['slab'=32,'rays'=8] {'slab'}, dimensions={0} | all-to-all | bytes 557056 | tf_op jit(solution)/shard_map/all_to_all | solution.py:397
  40.1 13.6 %bwd.1 = (f32[3,1,16]{2,1,0:T(1,128)}, f32[392,256]{1,0:T(8,128)S(1)}, f32[392,256]{1,0:T(8,128)S(1)}) custom-call(s32[3]{0:T(128)} %pad_add_fusion.refs_0_.ids_ref, f32[544,128]{1,0:T(8,128)S(1)} %bitcast.8, s32[1,1,512]{2,1,0:T(1,128)} %refs_2_.3, f32[1,256,256]{2,1,0:T(8,128)} %refs_3_.3, f32[1,2,256,256]{3,2,1,0:T(8,128)} %refs_4_.3, ...), custom_call_target="tpu_custom_call" | custom-call | tf_op jit(solution)/shard_map/bwd/pallas_call | solution.py:340
  53.7 0.0 copy-start
  53.7 2.2 %collective-permute-start = (f32[392,256]{1,0:T(8,128)S(1)}, f32[392,256]{1,0:T(8,128)S(1)}, u32[]{:S(2)}, u32[]{:S(2)}) collective-permute-start(f32[392,256]{1,0:T(8,128)S(1)} %get-tuple-element.42), channel_id=1, source_target_pairs={{0,1},{1,0},{2,3},{3,2},{4,5},{5,4},{6,7},{7,6},{8,9},{9,8},{10,11... | collective-permute-start | bytes 1204232 | tf_op jit(solution)/shard_map/ppermute | solution.py:401
  55.8 1.4 %collective-permute-done = f32[392,256]{1,0:T(8,128)S(1)} collective-permute-done((f32[392,256]{1,0:T(8,128)S(1)}, f32[392,256]{1,0:T(8,128)S(1)}, u32[]{:S(2)}, u32[]{:S(2)}) %collective-permute-start) | collective-permute-done | bytes 401440 | tf_op jit(solution)/shard_map/ppermute | solution.py:401
  57.2 0.1 add.12
  57.3 2.6 %collective-permute-start.3 = (f32[104,256]{1,0:T(8,128)S(1)}, f32[104,256]{1,0:T(8,128)S(1)}, u32[]{:S(2)}, u32[]{:S(2)}) collective-permute-start(f32[104,256]{1,0:T(8,128)S(1)} %concatenate.20), channel_id=1, source_target_pairs={{0,6},{1,7},{2,0},{3,1},{4,2},{5,3},{6,4},{7,5},{8,14},{9,15},{10,... | collective-permute-start | bytes 319496 | tf_op jit(solution)/shard_map/ppermute | solution.py:404
  59.9 0.1 collective-permute-start.1
  60.0 1.7 %collective-permute-start.2 = (f32[104,256]{1,0:T(8,128)S(1)}, f32[104,256]{1,0:T(8,128)S(1)}, u32[]{:S(2)}, u32[]{:S(2)}) collective-permute-start(f32[104,256]{1,0:T(8,128)S(1)} %get-tuple-element.52), channel_id=1, source_target_pairs={{0,4},{1,5},{2,6},{3,7},{4,0},{5,1},{6,2},{7,3},{8,12},{9,13},{10,... | collective-permute-start | bytes 319496 | tf_op jit(solution)/shard_map/ppermute | solution.py:404
  61.7 0.1 collective-permute-done.3
  61.8 5.9 %collective-permute-done.1 = f32[104,256]{1,0:T(8,128)S(1)} collective-permute-done((f32[104,256]{1,0:T(8,128)S(1)}, f32[104,256]{1,0:T(8,128)S(1)}, u32[]{:S(2)}, u32[]{:S(2)}) %collective-permute-start.1) | collective-permute-done | bytes 106528 | tf_op jit(solution)/shard_map/ppermute | solution.py:404
  67.7 0.0 collective-permute-done.2
  67.8 0.1 collective-permute-start.6
  67.8 0.3 collective-permute-start.5
  68.1 1.2 %collective-permute-start.4 = (f32[96,256]{1,0:T(8,128)S(1)}, f32[96,256]{1,0:T(8,128)S(1)}, u32[]{:S(2)}, u32[]{:S(2)}) collective-permute-start(f32[96,256]{1,0:T(8,128)S(1)} %slice.26), channel_id=1, source_target_pairs={{0,2},{1,3},{2,4},{3,5},{4,6},{5,7},{6,0},{7,1},{8,10},{9,11},{10,... | collective-permute-start | bytes 294920 | tf_op jit(solution)/shard_map/ppermute | solution.py:407
  69.3 2.0 %collective-permute-done.6.own3 = f32[96,256]{1,0:T(8,128)S(1)} collective-permute-done((f32[96,256]{1,0:T(8,128)S(1)}, f32[96,256]{1,0:T(8,128)S(1)}, u32[]{:S(2)}, u32[]{:S(2)}) %collective-permute-start.6) | collective-permute-done | bytes 98336 | tf_op jit(solution)/shard_map/ppermute | solution.py:407
  71.3 1.6 %collective-permute-done.5.own2 = f32[96,256]{1,0:T(8,128)S(1)} collective-permute-done((f32[96,256]{1,0:T(8,128)S(1)}, f32[96,256]{1,0:T(8,128)S(1)}, u32[]{:S(2)}, u32[]{:S(2)}) %collective-permute-start.5) | collective-permute-done | bytes 98336 | tf_op jit(solution)/shard_map/ppermute | solution.py:407
  72.9 1.0 %collective-permute-done.4.own1 = f32[96,256]{1,0:T(8,128)S(1)} collective-permute-done((f32[96,256]{1,0:T(8,128)S(1)}, f32[96,256]{1,0:T(8,128)S(1)}, u32[]{:S(2)}, u32[]{:S(2)}) %collective-permute-start.4) | collective-permute-done | bytes 98336 | tf_op jit(solution)/shard_map/ppermute | solution.py:407
  74.0 3.5 %collective-permute-start.7 = (f32[384,256]{1,0:T(8,128)S(1)}, f32[384,256]{1,0:T(8,128)S(1)}, u32[]{:S(2)}, u32[]{:S(2)}) collective-permute-start(f32[384,256]{1,0:T(8,128)S(1)} %pad_maximum_fusion), channel_id=1, source_target_pairs={{0,1},{1,0},{2,3},{3,2},{4,5},{5,4},{6,7},{7,6},{8,9},{9,8},{10,11... | collective-permute-start | bytes 1179656 | tf_op jit(solution)/shard_map/ppermute | solution.py:408
  77.5 1.3 %collective-permute-done.7.sib = f32[384,256]{1,0:T(8,128)S(1)} collective-permute-done((f32[384,256]{1,0:T(8,128)S(1)}, f32[384,256]{1,0:T(8,128)S(1)}, u32[]{:S(2)}, u32[]{:S(2)}) %collective-permute-start.7) | collective-permute-done | bytes 393248 | tf_op jit(solution)/shard_map/ppermute | solution.py:408
  78.8 0.0 copy-done
  78.8 1.5 %place.1 = (f32[1,256,256]{2,1,0:T(8,128)}, f32[1,2,256,256]{3,2,1,0:T(8,128)}, f32[1,4,256]{2,1,0:T(4,128)}, f32[3,1,256]{2,1,0:T(1,128)}, f32[1,4]{1,0:T(1,128)}) custom-call(s32[3]{0:T(128)S(1)} %copy-done, f32[104,256]{1,0:T(8,128)S(1)} %fusion.2.done, f32[96,256]{1,0:T(8,128)S(1)} %collective-permute-done.4.own1, ...), custom_call_target="tpu_custom_call" | custom-call | tf_op jit(solution)/shard_map/place/pallas_call | solution.py:376
  (7 shorter events, 0.1 us)
Async XLA Ops:
  53.7 25.1 %copy-start = (s32[3]{0:T(128)S(1)}, s32[3]{0:T(128)}, u32[]{:S(2)}) copy-start(s32[3]{0:T(128)} %pad_add_fusion.refs_0_.ids_ref) | copy-start | bytes 40
  53.7 3.5 %collective-permute-start = (f32[392,256]{1,0:T(8,128)S(1)}, f32[392,256]{1,0:T(8,128)S(1)}, u32[]{:S(2)}, u32[]{:S(2)}) collective-permute-start(f32[392,256]{1,0:T(8,128)S(1)} %get-tuple-element.42), channel_id=1, source_target_pairs={{0,1},{1,0},{2,3},{3,2},{4,5},{5,4},{6,7},{7,6},{8,9},{9,8},{10,11... | collective-permute-start | bytes 1204232 | tf_op jit(solution)/shard_map/ppermute | solution.py:401
  57.3 4.5 %collective-permute-start.3 = (f32[104,256]{1,0:T(8,128)S(1)}, f32[104,256]{1,0:T(8,128)S(1)}, u32[]{:S(2)}, u32[]{:S(2)}) collective-permute-start(f32[104,256]{1,0:T(8,128)S(1)} %concatenate.20), channel_id=1, source_target_pairs={{0,6},{1,7},{2,0},{3,1},{4,2},{5,3},{6,4},{7,5},{8,14},{9,15},{10,... | collective-permute-start | bytes 319496 | tf_op jit(solution)/shard_map/ppermute | solution.py:404
  59.9 7.8 %collective-permute-start.1 = (f32[104,256]{1,0:T(8,128)S(1)}, f32[104,256]{1,0:T(8,128)S(1)}, u32[]{:S(2)}, u32[]{:S(2)}) collective-permute-start(f32[104,256]{1,0:T(8,128)S(1)} %get-tuple-element.51), channel_id=1, source_target_pairs={{0,2},{1,3},{2,4},{3,5},{4,6},{5,7},{6,0},{7,1},{8,10},{9,11},{10,... | collective-permute-start | bytes 319496 | tf_op jit(solution)/shard_map/ppermute | solution.py:404
  60.0 7.7 %collective-permute-start.2 = (f32[104,256]{1,0:T(8,128)S(1)}, f32[104,256]{1,0:T(8,128)S(1)}, u32[]{:S(2)}, u32[]{:S(2)}) collective-permute-start(f32[104,256]{1,0:T(8,128)S(1)} %get-tuple-element.52), channel_id=1, source_target_pairs={{0,4},{1,5},{2,6},{3,7},{4,0},{5,1},{6,2},{7,3},{8,12},{9,13},{10,... | collective-permute-start | bytes 319496 | tf_op jit(solution)/shard_map/ppermute | solution.py:404
  67.8 3.5 %collective-permute-start.6 = (f32[96,256]{1,0:T(8,128)S(1)}, f32[96,256]{1,0:T(8,128)S(1)}, u32[]{:S(2)}, u32[]{:S(2)}) collective-permute-start(f32[96,256]{1,0:T(8,128)S(1)} %slice.26), channel_id=1, source_target_pairs={{0,6},{1,7},{2,0},{3,1},{4,2},{5,3},{6,4},{7,5},{8,14},{9,15},{10,... | collective-permute-start | bytes 294920 | tf_op jit(solution)/shard_map/ppermute | solution.py:407
  67.8 5.1 %collective-permute-start.5 = (f32[96,256]{1,0:T(8,128)S(1)}, f32[96,256]{1,0:T(8,128)S(1)}, u32[]{:S(2)}, u32[]{:S(2)}) collective-permute-start(f32[96,256]{1,0:T(8,128)S(1)} %slice.26), channel_id=1, source_target_pairs={{0,4},{1,5},{2,6},{3,7},{4,0},{5,1},{6,2},{7,3},{8,12},{9,13},{10,... | collective-permute-start | bytes 294920 | tf_op jit(solution)/shard_map/ppermute | solution.py:407
  68.1 5.8 %collective-permute-start.4 = (f32[96,256]{1,0:T(8,128)S(1)}, f32[96,256]{1,0:T(8,128)S(1)}, u32[]{:S(2)}, u32[]{:S(2)}) collective-permute-start(f32[96,256]{1,0:T(8,128)S(1)} %slice.26), channel_id=1, source_target_pairs={{0,2},{1,3},{2,4},{3,5},{4,6},{5,7},{6,0},{7,1},{8,10},{9,11},{10,... | collective-permute-start | bytes 294920 | tf_op jit(solution)/shard_map/ppermute | solution.py:407
  74.0 4.8 %collective-permute-start.7 = (f32[384,256]{1,0:T(8,128)S(1)}, f32[384,256]{1,0:T(8,128)S(1)}, u32[]{:S(2)}, u32[]{:S(2)}) collective-permute-start(f32[384,256]{1,0:T(8,128)S(1)} %pad_maximum_fusion), channel_id=1, source_target_pairs={{0,1},{1,0},{2,3},{3,2},{4,5},{5,4},{6,7},{7,6},{8,9},{9,8},{10,11... | collective-permute-start | bytes 1179656 | tf_op jit(solution)/shard_map/ppermute | solution.py:408

commit v2 on v1

--- a/solution.py
+++ b/solution.py
@@ -13,8 +13,10 @@
 RAYS = 512
 OWN = 16
 ROWS = 17
-SPB = 2
-STEPS = SAMP // SPB
+SF = 8
+SB = 8
+NF = SAMP // SF
+NB = SAMP // SB
 F32 = jnp.float32
 LOG2E = 1.4426950408889634
 LN2 = 0.6931471805599453
@@ -38,8 +40,7 @@
 def sincos(phase):
     turns = jnp.floor(phase * F32(2.0 / math.pi) + F32(0.5))
     r = phase - turns * F32(1.5703125)
-    r = r - turns * F32(4.837512969970703125e-4)
-    r = r - turns * F32(7.54978995489188216e-8)
+    r = r - turns * F32(math.pi / 2 - 1.5703125)
     z = r * r
     s = r + r * z * (F32(-1.6666654611e-1) + z * (F32(8.3321608736e-3) + z * F32(-1.9515295891e-4)))
     c = F32(1.0) - F32(0.5) * z + z * z * (
@@ -62,8 +63,8 @@
 
 def softplus2(x):
     v = jnp.exp2(jnp.minimum(x, F32(100.0)))
-    log = lax.log2(F32(1.0 - 2.0**-23) + v)
-    return jnp.maximum(jnp.maximum(log, v * (F32(LOG2E) - F32(0.5 * LOG2E) * v)), x)
+    log = lax.log2(F32(1.0 + 2.0**-23) + v)
+    return jnp.maximum(jnp.minimum(log, v * F32(LOG2E)), x)
 
 
 def sigmoid(x):
@@ -72,8 +73,8 @@
 
 
 def forward_kernel(
-    me_ref, geo_ref, entry_ref, counts_ref, tgt_ref, win_ref, wmid_ref, wout_ref, bhid_ref, bout_ref, freqs_ref,
-    send_ref, out_ref, fh_ref, fl_ref, h1h_ref, h1l_ref, h2h_ref, h2l_ref, h3h_ref, h3l_ref, s1_ref, s2_ref, s3_ref,
+    geo_ref, entry_ref, counts_ref, tgt_ref, win_ref, wmid_ref, wout_ref, bhid_ref, bout_ref, freqs_ref,
+    send_ref, wb_ref, wob_ref, out_ref, fh_ref, fl_ref, h1h_ref, h1l_ref, h2h_ref, h2l_ref, h3h_ref, h3l_ref, s1_ref, s2_ref, s3_ref,
     wcat, wo, bias, rot, feat, before, color,
     *, delta,
 ):
@@ -91,6 +92,15 @@
         w8 = jnp.concatenate([wout_ref[0] * F32(LN2), jnp.zeros((4, H), F32)], axis=0)
         hi, lo = split(w8)
         wo[...] = jnp.concatenate([hi.astype(F32), lo.astype(F32)], axis=0).astype(BF16)
+        for i in range(2):
+            hi, lo = split(wmid_ref[0, i])
+            wb_ref[i, :, 0:256] = hi
+            wb_ref[i, :, 256:512] = hi
+            wb_ref[i, :, 512:768] = lo
+        w8 = jnp.concatenate([wout_ref[0], jnp.zeros((4, H), F32)], axis=0)
+        hi, lo = split(w8)
+        hi, lo = hi.astype(F32), lo.astype(F32)
+        wob_ref[...] = jnp.concatenate([hi, hi, lo, jnp.zeros((104, H), F32)], axis=0).T[:, 0:32].astype(BF16)
         ft = jnp.concatenate([freqs_ref[0], freqs_ref[1], freqs_ref[2], jnp.zeros((5, FE), F32)], axis=0).T
         geo = geo_ref[:, 0, :]
         a = ft[:, 0:1] * geo[0:1] + ft[:, 1:2] * geo[1:2] + ft[:, 2:3] * geo[2:3]
@@ -105,7 +115,7 @@
         before[...] = jnp.zeros_like(before)
         color[...] = jnp.zeros_like(color)
 
-    n = step * SPB
+    n = step * SF
 
     def slot_input(j):
         s, c = feat[0:FE], feat[FE:]
@@ -115,11 +125,11 @@
         feat[0:FE] = s * rc + c * rs
         feat[FE:] = c * rc - s * rs
 
-    for j in range(SPB):
+    for j in range(SF):
         slot_input(j)
     srcs = [(fh_ref, fl_ref), (h1h_ref, h1l_ref), (h2h_ref, h2l_ref), (h3h_ref, h3l_ref)]
     sigs = [s1_ref, s2_ref, s3_ref]
-    parts = [(j, k) for j in range(SPB) for k in range(2)]
+    parts = [(j, k) for j in range(SF) for k in range(2)]
     for i in range(3):
         b = jnp.concatenate([bias[i], bias[i]], axis=1)
         for j, k in parts:
@@ -132,23 +142,24 @@
             srcs[i + 1][0][n + j, :, lanes], srcs[i + 1][1][n + j, :, lanes] = split(h)
     bo = jnp.concatenate([bout_ref[0:1, :], jnp.zeros((1, 124), F32)], axis=1)
     bo = jnp.broadcast_to(bo, (128, 128)).T[0:8, 0:1]
-    for j in range(SPB):
+    for j in range(SF):
         d1 = mm(wo[...], h3h_ref[n + j])
         d2 = mm(wo[...], h3l_ref[n + j])
         o = d1[0:8] + d1[8:16] + d2[0:8] + d2[8:16] + bo
-        out_ref[step * SPB + j] = o
-        alive = step * SPB + j < counts_ref[0]
-        depth = jnp.where(alive, softplus(o[0:1]) * F32(delta), F32(0.0))
+        gate = jnp.where(step * SF + j < counts_ref[0], F32(delta), F32(0.0))
+        depth = softplus(o[0:1]) * gate
         bef = before[...]
         w = jnp.exp(-bef) * (F32(1.0) - jnp.exp(-depth))
-        color[...] += w * sigmoid(o)
+        sg = sigmoid(o)
+        color[...] += w * sg
         before[...] = bef + depth
-
-    @pl.when(step == STEPS - 1)
+        out_ref[step * SF + j] = jnp.concatenate([sg[0:4], w, jnp.exp(-(bef + depth)), gate, jnp.zeros_like(w)], axis=0)
+
+    @pl.when(step == NF - 1)
     def _():
         t = tgt_ref[:, 0, :]
         t = jnp.concatenate([t[0:1], t[1:2], t[2:3], jnp.zeros((1, 80), F32)], axis=1)
-        t = pltpu.roll(jnp.broadcast_to(t, (8, 128)), lax.rem(me_ref[0], 8) * OWN, 1)[0:1]
+        t = pltpu.roll(jnp.broadcast_to(t, (8, 128)), lax.rem(lax.axis_index("slab"), 8) * OWN, 1)[0:1]
         rows = []
         for c in range(4):
             v = color[c + 1 : c + 2] if c < 3 else -before[...]
@@ -159,6 +170,11 @@
             send_ref[s * ROWS : (s + 1) * ROWS] = value
 
 
+def where():
+    ray = lax.axis_index("rays")
+    return lax.rem(ray, 2), lax.div(ray, 2)
+
+
 def keep(x):
     return pltpu.with_memory_space_constraint(x, pltpu.VMEM)
 
@@ -171,18 +187,14 @@
     return pl.BlockSpec(shape, lambda i, n=len(shape): (0,) * n)
 
 
-def smem():
-    return pl.BlockSpec(memory_space=pltpu.SMEM)
-
-
-def forward(me, geo, entry, counts, tgt, w_in, w_mid, w_out, b_hid, b_out, freqs, delta):
-    res = [jax.ShapeDtypeStruct((32 * ROWS, 128), F32), pltpu.VMEM((SAMP, 8, RAYS), F32)]
+def forward(geo, entry, counts, tgt, w_in, w_mid, w_out, b_hid, b_out, freqs, delta):
+    res = [jax.ShapeDtypeStruct((32 * ROWS, 128), F32), pltpu.VMEM((2, H, 3 * H), BF16), pltpu.VMEM((H, 32), BF16), pltpu.VMEM((SAMP, 8, RAYS), F32)]
     res += [pltpu.VMEM((SAMP, H, RAYS), BF16)] * 8 + [pltpu.VMEM((SAMP, H, RAYS), F32)] * 3
     return pl.pallas_call(
         lambda *refs: forward_kernel(*refs, delta=delta),
-        grid=(STEPS,),
-        in_specs=[smem()] + [full(x.shape) for x in (geo, entry, counts, tgt, w_in, w_mid, w_out, b_hid, b_out, freqs)],
-        out_specs=[full((32 * ROWS, 128)), vmem()] + [vmem()] * 11,
+        grid=(NF,),
+        in_specs=[full(x.shape) for x in (geo, entry, counts, tgt, w_in, w_mid, w_out, b_hid, b_out, freqs)],
+        out_specs=[full((32 * ROWS, 128))] + [vmem()] * 14,
         out_shape=res,
         scratch_shapes=[
             pltpu.VMEM((3, H, 3 * H), BF16), pltpu.VMEM((16, H), BF16),
@@ -191,30 +203,21 @@
         ],
         compiler_params=pltpu.CompilerParams(vmem_limit_bytes=28 * 1024 * 1024),
         name="fwd",
-    )(me, geo, entry, counts, tgt, w_in, w_mid, w_out, b_hid, b_out, freqs)
+    )(geo, entry, counts, tgt, w_in, w_mid, w_out, b_hid, b_out, freqs)
 
 
 def backward_kernel(
-    me_ref, recv_ref, counts_ref, win_ref, wmid_ref, wout_ref, out_ref,
+    recv_ref, wcat, wo, out_ref,
     fh_ref, fl_ref, h1h_ref, h1l_ref, h2h_ref, h2l_ref, h3h_ref, h3l_ref, s1_ref, s2_ref, s3_ref,
     pix_ref, mine_ref, other_ref,
-    wcat, wo, g_all, adj, pixs, acc, bacc, gacc, goacc, dh_buf,
-    *, delta, factor,
+    g_all, adj, pixs, acc, bacc, gacc, goacc, dh_buf,
+    *, factor,
 ):
     step = pl.program_id(0)
 
     @pl.when(step == 0)
     def _():
-        me = me_ref[0]
-        for i in range(2):
-            hi, lo = split(wmid_ref[0, i])
-            wcat[i, :, 0:256] = hi
-            wcat[i, :, 256:512] = hi
-            wcat[i, :, 512:768] = lo
-        w8 = jnp.concatenate([wout_ref[0], jnp.zeros((4, H), F32)], axis=0)
-        hi, lo = split(w8)
-        hi, lo = hi.astype(F32), lo.astype(F32)
-        wo[...] = jnp.concatenate([hi, hi, lo, jnp.zeros((104, H), F32)], axis=0).T[:, 0:32].astype(BF16)
+        me = lax.axis_index("slab")
         acc[...] = jnp.zeros_like(acc)
         bacc[...] = jnp.zeros_like(bacc)
         gacc[...] = jnp.zeros_like(gacc)
@@ -259,27 +262,19 @@
             pix_ref[c] = row[0:1, 0:OWN]
         log_adj = jnp.concatenate([log_adj[q : q + 1] for q in range(4)], axis=1)
         a8 = adj[...]
-        counts = counts_ref[0]
-        bef = jnp.zeros((1, RAYS), F32)
-        ends, weights = [], []
-        for j in range(SAMP):
-            dep = jnp.where(j < counts, softplus(out_ref[j, 0:1]) * F32(delta), F32(0.0))
-            weights.append(jnp.exp(-bef) * (F32(1.0) - jnp.exp(-dep)))
-            bef = bef + dep
-            ends.append(jnp.exp(-bef))
         later = jnp.zeros((8, RAYS), F32)
         first = lax.broadcasted_iota(jnp.int32, (8, RAYS), 0) == 0
         for j in reversed(range(SAMP)):
-            sg = sigmoid(out_ref[j])
-            ddep = jnp.sum(a8 * (ends[j] * sg - later), axis=0, keepdims=True) - log_adj
-            ddep = jnp.where(j < counts, F32(delta) * ddep, F32(0.0))
-            g = jnp.where(first, ddep * sg, a8 * weights[j] * (sg * (F32(1.0) - sg)))
-            later = later + weights[j] * sg
+            sg = out_ref[j]
+            w, end, gate = sg[4:5], sg[5:6], sg[6:7]
+            ddep = gate * (jnp.sum(a8 * (end * sg - later), axis=0, keepdims=True) - log_adj)
+            g = jnp.where(first, ddep * sg, a8 * w * (sg * (F32(1.0) - sg)))
+            later = later + w * sg
             g_all[j] = g
 
-    n = step * SPB
-    for j in range(SPB):
-        g = g_all[step * SPB + j]
+    n = step * SB
+    for j in range(SB):
+        g = g_all[step * SB + j]
         gacc[...] += g[:, 0:128] + g[:, 128:256] + g[:, 256:384] + g[:, 384:512]
         gb = [[jnp.broadcast_to(g[c : c + 1, 128 * t : 128 * t + 128], (8, 128)) for t in range(4)] for c in range(4)]
         for r in range(0, H, 16):
@@ -301,7 +296,7 @@
     hs = ((h2h_ref, h2l_ref), (h1h_ref, h1l_ref), (fh_ref, fl_ref))
     for i in range(3):
         lhs, rhs = [], []
-        for j in range(SPB):
+        for j in range(SB):
             dx = dh_buf[j] * sigs[i][n + j]
             bacc[2 - i] += dx[:, 0:128] + dx[:, 128:256] + dx[:, 256:384] + dx[:, 384:512]
             xh, xl = split(dx)
@@ -311,9 +306,9 @@
                 dh_buf[j] = mm(wcat[1 - i], jnp.concatenate([xh, xl, xh], axis=0))
         acc[2 - i] += mm_nt(jnp.concatenate(lhs, axis=1), jnp.concatenate(rhs, axis=1))
 
-    @pl.when(step == STEPS - 1)
+    @pl.when(step == NB - 1)
     def _():
-        core, chip = me_ref[1], me_ref[2]
+        core, chip = where()
         for k in range(4):
             q = lax.rem(chip + k, 4)
             for i in range(3):
@@ -333,69 +328,94 @@
         other_ref[384:392] = small
 
 
-def backward(ids, recv, counts, w_in, w_mid, w_out, out, residuals, delta, factor):
-    half = pltpu.VMEM((392, H), F32)
-    recv, out = keep(recv), keep(out)
-    residuals = [keep(x) for x in residuals]
+def backward(recv, wb, wo, out, residuals, factor):
+    args = [keep(x) for x in (recv, wb, wo, out, *residuals)]
     return pl.pallas_call(
-        lambda *refs: backward_kernel(*refs, delta=delta, factor=factor),
-        grid=(STEPS,),
-        in_specs=[smem(), vmem()] + [full(x.shape) for x in (counts, w_in, w_mid, w_out)] + [vmem()] + [vmem()] * 11,
-        out_specs=[full((3, 1, OWN)), vmem(), vmem()],
-        out_shape=[jax.ShapeDtypeStruct((3, 1, OWN), F32), half, half],
+        lambda *refs: backward_kernel(*refs, factor=factor),
+        grid=(NB,),
+        in_specs=[vmem()] * len(args),
+        out_specs=[vmem()] * 3,
+        out_shape=[pltpu.VMEM((3, 1, OWN), F32), pltpu.VMEM((392, H), F32), pltpu.VMEM((392, H), F32)],
         scratch_shapes=[
-            pltpu.VMEM((2, H, 3 * H), BF16), pltpu.VMEM((H, 32), BF16),
             pltpu.VMEM((SAMP, 8, RAYS), F32), pltpu.VMEM((8, RAYS), F32), pltpu.VMEM((16, 128), F32),
             pltpu.VMEM((3, H, H), F32), pltpu.VMEM((3, H, 128), F32), pltpu.VMEM((8, 128), F32), pltpu.VMEM((4, H, 128), F32),
-            pltpu.VMEM((SPB, H, RAYS), F32),
+            pltpu.VMEM((SB, H, RAYS), F32),
         ],
-        compiler_params=pltpu.CompilerParams(vmem_limit_bytes=28 * 1024 * 1024),
+        compiler_params=pltpu.CompilerParams(vmem_limit_bytes=24 * 1024 * 1024),
         name="bwd",
-    )(ids, recv, counts, w_in, w_mid, w_out, out, *residuals)
-
-
-def place_kernel(ids_ref, done, own1, own2, own3, sib, gin, gmid, gout, ghid, gbout):
-    own = (done, own1, own2, own3)
-    core, chip = ids_ref[1], ids_ref[2]
+    )(*args)
+
+
+def copies(side, sources, gin, gmid, sem):
+    core, chip = where()
+    started = []
     for k in range(4):
         q = lax.rem(chip + 4 - k, 4)
-        for side in range(2):
-            src, base = (own[k], 0) if side == 0 else (sib, 96 * k)
-            rows = pl.ds(((core if side == 0 else 1 - core) * 4 + q) * 32, 32)
-            gin[0, rows] = src[base : base + 32]
-            gmid[0, 0, rows] = src[base + 32 : base + 64]
-            gmid[0, 1, rows] = src[base + 64 : base + 96]
+        rows = pl.ds(((core if side == 0 else 1 - core) * 4 + q) * 32, 32)
+        src, base = sources(k)
+        for i, dst in enumerate((gin.at[0, rows], gmid.at[0, 0, rows], gmid.at[0, 1, rows])):
+            copy = pltpu.make_async_copy(src.at[pl.ds(base + 32 * i, 32)], dst, sem.at[3 * k + i])
+            copy.start()
+            started.append(copy)
+    return started
+
+
+def place_own_kernel(done, own1, own2, own3, gin, gmid, gout, ghid, gbout, sem):
+    own = (done, own1, own2, own3)
+    started = copies(0, lambda k: (own[k], 0), gin, gmid, sem)
     gout[0] = done[96:100]
     for i in range(3):
         ghid[i] = done[100 + i : 101 + i]
     gbout[...] = done[103:104, 0:4]
-
-
-def place(ids, done, own, sib):
+    for copy in started:
+        copy.wait()
+
+
+def place_other_kernel(sib, gin_in, gmid_in, gin, gmid, sem):
+    for copy in copies(1, lambda k: (sib, 96 * k), gin, gmid, sem):
+        copy.wait()
+
+
+def hbm():
+    return pl.BlockSpec(memory_space=pl.ANY)
+
+
+def place_own(done, own):
     shapes = [(1, H, H), (1, 2, H, H), (1, 4, H), (3, 1, H), (1, 4)]
     return pl.pallas_call(
-        place_kernel,
-        in_specs=[smem()] + [vmem()] * 5,
-        out_specs=[vmem()] * 5,
+        place_own_kernel,
+        in_specs=[vmem()] * 4,
+        out_specs=[hbm()] * 2 + [vmem()] * 3,
         out_shape=[jax.ShapeDtypeStruct(x, F32) for x in shapes],
+        scratch_shapes=[pltpu.SemaphoreType.DMA((12,))],
         compiler_params=pltpu.CompilerParams(vmem_limit_bytes=16 * 1024 * 1024),
-        name="place",
-    )(ids, *[keep(x) for x in (done, *own, sib)])
+        name="place_own",
+    )(*[keep(x) for x in (done, *own)])
+
+
+def place_other(sib, gin, gmid):
+    return pl.pallas_call(
+        place_other_kernel,
+        in_specs=[vmem()] + [hbm()] * 2,
+        out_specs=[hbm()] * 2,
+        out_shape=[jax.ShapeDtypeStruct(x.shape, F32) for x in (gin, gmid)],
+        scratch_shapes=[pltpu.SemaphoreType.DMA((12,))],
+        input_output_aliases={1: 0, 2: 1},
+        compiler_params=pltpu.CompilerParams(vmem_limit_bytes=16 * 1024 * 1024),
+        name="place_other",
+    )(keep(sib), gin, gmid)
 
 
 def shards(geometry, entry, counts, targets, w_in, w_mid, w_out, b_hid, b_out, freqs):
     slabs = lax.axis_size("slab")
     delta = 3.0 / (SAMP * slabs)
     factor = 1.0 / math.sqrt(3.0 * lax.axis_size("rays") * slabs * OWN)
-    me = lax.axis_index("slab")
-    ray = lax.axis_index("rays")
-    ids = jnp.stack([me, lax.rem(ray, 2), lax.div(ray, 2)]).astype(jnp.int32)
-    send, out, *residuals = forward(
-        ids, geometry, entry, counts, targets, w_in, w_mid, w_out,
+    send, wb, wo, out, *residuals = forward(
+        geometry, entry, counts, targets, w_in, w_mid, w_out,
         b_hid.transpose(1, 0, 2), b_out, freqs.transpose(1, 0, 2), delta
     )
     recv = lax.all_to_all(send.reshape(32, 1, ROWS * 128), "slab", 0, 0, tiled=True).reshape(32 * ROWS, 128)
-    pixels, mine, other = backward(ids, recv, counts, w_in, w_mid, w_out, out, residuals, delta, factor)
+    pixels, mine, other = backward(recv, wb, wo, out, residuals, factor)
     swap = [(i, i ^ 1) for i in range(8)]
     along = [[(i, (i + 2 * k) % 8) for i in range(8)] for k in range(4)]
     total = mine + lax.ppermute(other, "rays", swap)
@@ -406,7 +426,8 @@
     chunk = done[0:96]
     own = [lax.ppermute(chunk, "rays", along[k]) for k in range(1, 4)]
     sib = lax.ppermute(jnp.concatenate([chunk] + own, axis=0), "rays", swap)
-    grad_in, grad_mid, grad_out, grad_hid, grad_bout = place(ids, done, own, sib)
+    grad_in, grad_mid, grad_out, grad_hid, grad_bout = place_own(done, own)
+    grad_in, grad_mid = place_other(sib, grad_in, grad_mid)
     return pixels, grad_in, grad_mid, grad_out, grad_hid.transpose(1, 0, 2), grad_bout
 
 

time: 80.5 us -> 73.7 us (0.916)
  Pallas kernels: 30.1 us -> 24.2 us
  waiting for transfers between devices: 13.3 us -> 12 us
    pallas_call x3 -> x4, Pallas kernels: 30.1 us -> 24.2 us  [the longest x1 11 us: backward(): pl.pallas_call(lambda *refs: backward_kernel(*refs, factor=factor), grid=...]
    ppermute x1, waiting for transfers between devices: 1.35 us -> 0.01 us  [shards(): sib = lax.ppermute(jnp.concatenate([chunk] + own, axis=0), 'rays', swap)]
  transfers between devices with their start and end apart: 8 -> 8, of which waited for: 7 -> 5; matrix products, arithmetic and copies ran while one was open for 0% -> 1% of each run, Pallas kernels for 0% -> 2%
where the time goes in v2:
time: 73.7 us; the launch traced here: 73.5 us
  Pallas kernels  24.2 us (33%)
  blocking collectives  23.8 us (32%)
  waiting for transfers between devices  12 us (16%)
  starting transfers between devices  11.8 us (16%)
  between operations  0.91 us (1%)
    all_to_all x1, blocking collectives, shards(): lax.all_to_all(send.reshape(32, 1, ROWS * 128), 'slab', 0, 0, tiled=True)  23.8 us
    pallas_call x1, Pallas kernels, backward(): pl.pallas_call(lambda *refs: backward_kernel(*refs, factor=factor), grid=...  11 us
    pallas_call x1, Pallas kernels, forward(): pl.pallas_call(lambda *refs: forward_kernel(*refs, delta=delta), grid=(NF...  10.9 us
    ppermute x3, waiting for transfers between devices, shards(): got = [lax.ppermute(parts[k], 'rays', along[k]) for k in range(1, 4)]  5.99 us
    ppermute x3, waiting for transfers between devices, shards(): own = [lax.ppermute(chunk, 'rays', along[k]) for k in range(1, 4)]  4.65 us
    ppermute x3, starting transfers between devices, shards(): got = [lax.ppermute(parts[k], 'rays', along[k]) for k in range(1, 4)]  4.58 us
    ppermute x1, starting transfers between devices, shards(): sib = lax.ppermute(jnp.concatenate([chunk] + own, axis=0), 'rays', swap)  3.46 us
    ppermute x1, starting transfers between devices, shards(): total = mine + lax.ppermute(other, 'rays', swap)  2.27 us
  transfers between devices with their start and end apart: 8, of which 5 were waited for; matrix products, arithmetic and copies ran while one was open for 1% of the time, Pallas kernels for 2%

profile of v2, /device:TPU:1, one launch (start us, length us, event | category | flops | bytes accessed | tf_op | source)
XLA Modules:
  0.0 73.5 jit_solution(16839888748189183085)
XLA Ops:
  0.6 10.9 %fwd.1 = (f32[544,128]{1,0:T(8,128)}, bf16[2,256,768]{2,1,0:T(8,128)(2,1)S(1)}, bf16[256,32]{1,0:T(8,128)(2,1)S(1)}, f32[8,8,512]{2,1,0:T(8,128)S(1)}, bf16[8,25...) custom-call(f32[6,1,512]{2,1,0:T(1,128)} %refs_0_.1, ...), custom_call_target="tpu_custom_call" | custom-call | tf_op jit(solution)/shard_map/fwd/pallas_call | solution.py:193
  11.6 23.8 %all_to_all.5 = f32[32,1,2176]{2,1,0:T(1,128)S(1)} all-to-all(f32[32,1,2176]{2,1,0:T(1,128)} %bitcast.6), channel_id=1, replica_groups=mesh['slab'=32,'rays'=8] {'slab'}, dimensions={0} | all-to-all | bytes 557056 | tf_op jit(solution)/shard_map/all_to_all | solution.py:417
  35.4 11.0 %bwd.1 = (f32[3,1,16]{2,1,0:T(1,128)S(1)}, f32[392,256]{1,0:T(8,128)S(1)}, f32[392,256]{1,0:T(8,128)S(1)}) custom-call(f32[544,128]{1,0:T(8,128)S(1)} %bitcast.5, bf16[2,256,768]{2,1,0:T(8,128)(2,1)S(1)} %get-tuple-element.32.refs_1_, bf16[256,32]{1,0:T(8,128)(2,1)S(1)} %get-tuple-element.33.refs_2_, f32[8,8,512]{2,1,0:T(8,128)S(1)} %get-tuple-element.34.refs_3_, ...), custom_call_target="tpu_custom_call" | custom-call | tf_op jit(solution)/shard_map/bwd/pallas_call | solution.py:333
  46.4 2.3 %collective-permute-start = (f32[392,256]{1,0:T(8,128)S(1)}, f32[392,256]{1,0:T(8,128)S(1)}, u32[]{:S(2)}, u32[]{:S(2)}) collective-permute-start(f32[392,256]{1,0:T(8,128)S(1)} %get-tuple-element.48), channel_id=1, source_target_pairs={{0,1},{1,0},{2,3},{3,2},{4,5},{5,4},{6,7},{7,6},{8,9},{9,8},{10,11... | collective-permute-start | bytes 1204232 | tf_op jit(solution)/shard_map/ppermute | solution.py:421
  48.7 1.4 %collective-permute-done = f32[392,256]{1,0:T(8,128)S(1)} collective-permute-done((f32[392,256]{1,0:T(8,128)S(1)}, f32[392,256]{1,0:T(8,128)S(1)}, u32[]{:S(2)}, u32[]{:S(2)}) %collective-permute-start) | collective-permute-done | bytes 401440 | tf_op jit(solution)/shard_map/ppermute | solution.py:421
  50.0 0.1 add.12
  50.1 2.6 %collective-permute-start.3 = (f32[104,256]{1,0:T(8,128)S(1)}, f32[104,256]{1,0:T(8,128)S(1)}, u32[]{:S(2)}, u32[]{:S(2)}) collective-permute-start(f32[104,256]{1,0:T(8,128)S(1)} %concatenate.20), channel_id=1, source_target_pairs={{0,6},{1,7},{2,0},{3,1},{4,2},{5,3},{6,4},{7,5},{8,14},{9,15},{10,... | collective-permute-start | bytes 319496 | tf_op jit(solution)/shard_map/ppermute | solution.py:424
  52.7 0.3 collective-permute-start.1
  53.0 1.7 %collective-permute-start.2 = (f32[104,256]{1,0:T(8,128)S(1)}, f32[104,256]{1,0:T(8,128)S(1)}, u32[]{:S(2)}, u32[]{:S(2)}) collective-permute-start(f32[104,256]{1,0:T(8,128)S(1)} %get-tuple-element.60), channel_id=1, source_target_pairs={{0,4},{1,5},{2,6},{3,7},{4,0},{5,1},{6,2},{7,3},{8,12},{9,13},{10,... | collective-permute-start | bytes 319496 | tf_op jit(solution)/shard_map/ppermute | solution.py:424
  54.8 0.0 collective-permute-done.3
  54.8 6.0 %collective-permute-done.1 = f32[104,256]{1,0:T(8,128)S(1)} collective-permute-done((f32[104,256]{1,0:T(8,128)S(1)}, f32[104,256]{1,0:T(8,128)S(1)}, u32[]{:S(2)}, u32[]{:S(2)}) %collective-permute-start.1) | collective-permute-done | bytes 106528 | tf_op jit(solution)/shard_map/ppermute | solution.py:424
  60.7 0.0 collective-permute-done.2
  60.8 0.1 collective-permute-start.6
  60.9 0.3 collective-permute-start.5
  61.2 1.2 %collective-permute-start.4 = (f32[96,256]{1,0:T(8,128)S(1)}, f32[96,256]{1,0:T(8,128)S(1)}, u32[]{:S(2)}, u32[]{:S(2)}) collective-permute-start(f32[96,256]{1,0:T(8,128)S(1)} %slice.26), channel_id=1, source_target_pairs={{0,2},{1,3},{2,4},{3,5},{4,6},{5,7},{6,0},{7,1},{8,10},{9,11},{10,... | collective-permute-start | bytes 294920 | tf_op jit(solution)/shard_map/ppermute | solution.py:427
  62.3 2.0 %collective-permute-done.6.own3 = f32[96,256]{1,0:T(8,128)S(1)} collective-permute-done((f32[96,256]{1,0:T(8,128)S(1)}, f32[96,256]{1,0:T(8,128)S(1)}, u32[]{:S(2)}, u32[]{:S(2)}) %collective-permute-start.6) | collective-permute-done | bytes 98336 | tf_op jit(solution)/shard_map/ppermute | solution.py:427
  64.3 1.6 %collective-permute-done.5.own2 = f32[96,256]{1,0:T(8,128)S(1)} collective-permute-done((f32[96,256]{1,0:T(8,128)S(1)}, f32[96,256]{1,0:T(8,128)S(1)}, u32[]{:S(2)}, u32[]{:S(2)}) %collective-permute-start.5) | collective-permute-done | bytes 98336 | tf_op jit(solution)/shard_map/ppermute | solution.py:427
  66.0 1.0 %collective-permute-done.4.own1 = f32[96,256]{1,0:T(8,128)S(1)} collective-permute-done((f32[96,256]{1,0:T(8,128)S(1)}, f32[96,256]{1,0:T(8,128)S(1)}, u32[]{:S(2)}, u32[]{:S(2)}) %collective-permute-start.4) | collective-permute-done | bytes 98336 | tf_op jit(solution)/shard_map/ppermute | solution.py:427
  67.0 3.5 %collective-permute-start.7 = (f32[384,256]{1,0:T(8,128)S(1)}, f32[384,256]{1,0:T(8,128)S(1)}, u32[]{:S(2)}, u32[]{:S(2)}) collective-permute-start(f32[384,256]{1,0:T(8,128)S(1)} %pad_maximum_fusion), channel_id=1, source_target_pairs={{0,1},{1,0},{2,3},{3,2},{4,5},{5,4},{6,7},{7,6},{8,9},{9,8},{10,11... | collective-permute-start | bytes 1179656 | tf_op jit(solution)/shard_map/ppermute | solution.py:428
  70.5 0.6 copy.21
  71.1 1.4 %place_own.1 = (f32[1,256,256]{2,1,0:T(8,128)}, f32[1,2,256,256]{3,2,1,0:T(8,128)}, f32[1,4,256]{2,1,0:T(4,128)}, f32[3,1,256]{2,1,0:T(1,128)}, f32[1,4]{1,0:T(1,128)}) custom-call(f32[104,256]{1,0:T(8,128)S(1)} %fusion.2.done, f32[96,256]{1,0:T(8,128)S(1)} %collective-permute-done.4.own1, f32[96,256]{1,0:T(8,128)S(1)} %collective-permute-done.5.own2, ...), custom_call_target="tpu_custom_call" | custom-call | tf_op jit(solution)/shard_map/place_own/pallas_call | solution.py:385
  72.5 0.0 collective-permute-done.7.sib
  72.5 0.9 %place_other.1 = (f32[1,256,256]{2,1,0:T(8,128)}, f32[1,2,256,256]{3,2,1,0:T(8,128)}) custom-call(f32[384,256]{1,0:T(8,128)S(1)} %collective-permute-done.7.sib, f32[1,256,256]{2,1,0:T(8,128)} %get-tuple-element.49.gin_in, f32[1,2,256,256]{3,2,1,0:T(8,128)} %get-tuple-element.50.gmid_in), custom_call_target="tpu_custom_call", output_to_operand_aliasing={{0}: (1, {}), {1}: (2, {})} | custom-call | tf_op jit(solution)/shard_map/place_other/pallas_call | solution.py:397
  (7 shorter events, 0.1 us)
Async XLA Ops:
  46.4 3.6 %collective-permute-start = (f32[392,256]{1,0:T(8,128)S(1)}, f32[392,256]{1,0:T(8,128)S(1)}, u32[]{:S(2)}, u32[]{:S(2)}) collective-permute-start(f32[392,256]{1,0:T(8,128)S(1)} %get-tuple-element.48), channel_id=1, source_target_pairs={{0,1},{1,0},{2,3},{3,2},{4,5},{5,4},{6,7},{7,6},{8,9},{9,8},{10,11... | collective-permute-start | bytes 1204232 | tf_op jit(solution)/shard_map/ppermute | solution.py:421
  50.1 4.6 %collective-permute-start.3 = (f32[104,256]{1,0:T(8,128)S(1)}, f32[104,256]{1,0:T(8,128)S(1)}, u32[]{:S(2)}, u32[]{:S(2)}) collective-permute-start(f32[104,256]{1,0:T(8,128)S(1)} %concatenate.20), channel_id=1, source_target_pairs={{0,6},{1,7},{2,0},{3,1},{4,2},{5,3},{6,4},{7,5},{8,14},{9,15},{10,... | collective-permute-start | bytes 319496 | tf_op jit(solution)/shard_map/ppermute | solution.py:424
  52.7 8.0 %collective-permute-start.1 = (f32[104,256]{1,0:T(8,128)S(1)}, f32[104,256]{1,0:T(8,128)S(1)}, u32[]{:S(2)}, u32[]{:S(2)}) collective-permute-start(f32[104,256]{1,0:T(8,128)S(1)} %get-tuple-element.59), channel_id=1, source_target_pairs={{0,2},{1,3},{2,4},{3,5},{4,6},{5,7},{6,0},{7,1},{8,10},{9,11},{10,... | collective-permute-start | bytes 319496 | tf_op jit(solution)/shard_map/ppermute | solution.py:424
  53.0 7.7 %collective-permute-start.2 = (f32[104,256]{1,0:T(8,128)S(1)}, f32[104,256]{1,0:T(8,128)S(1)}, u32[]{:S(2)}, u32[]{:S(2)}) collective-permute-start(f32[104,256]{1,0:T(8,128)S(1)} %get-tuple-element.60), channel_id=1, source_target_pairs={{0,4},{1,5},{2,6},{3,7},{4,0},{5,1},{6,2},{7,3},{8,12},{9,13},{10,... | collective-permute-start | bytes 319496 | tf_op jit(solution)/shard_map/ppermute | solution.py:424
  60.8 3.5 %collective-permute-start.6 = (f32[96,256]{1,0:T(8,128)S(1)}, f32[96,256]{1,0:T(8,128)S(1)}, u32[]{:S(2)}, u32[]{:S(2)}) collective-permute-start(f32[96,256]{1,0:T(8,128)S(1)} %slice.26), channel_id=1, source_target_pairs={{0,6},{1,7},{2,0},{3,1},{4,2},{5,3},{6,4},{7,5},{8,14},{9,15},{10,... | collective-permute-start | bytes 294920 | tf_op jit(solution)/shard_map/ppermute | solution.py:427
  60.9 5.1 %collective-permute-start.5 = (f32[96,256]{1,0:T(8,128)S(1)}, f32[96,256]{1,0:T(8,128)S(1)}, u32[]{:S(2)}, u32[]{:S(2)}) collective-permute-start(f32[96,256]{1,0:T(8,128)S(1)} %slice.26), channel_id=1, source_target_pairs={{0,4},{1,5},{2,6},{3,7},{4,0},{5,1},{6,2},{7,3},{8,12},{9,13},{10,... | collective-permute-start | bytes 294920 | tf_op jit(solution)/shard_map/ppermute | solution.py:427
  61.2 5.8 %collective-permute-start.4 = (f32[96,256]{1,0:T(8,128)S(1)}, f32[96,256]{1,0:T(8,128)S(1)}, u32[]{:S(2)}, u32[]{:S(2)}) collective-permute-start(f32[96,256]{1,0:T(8,128)S(1)} %slice.26), channel_id=1, source_target_pairs={{0,2},{1,3},{2,4},{3,5},{4,6},{5,7},{6,0},{7,1},{8,10},{9,11},{10,... | collective-permute-start | bytes 294920 | tf_op jit(solution)/shard_map/ppermute | solution.py:427
  67.0 5.5 %collective-permute-start.7 = (f32[384,256]{1,0:T(8,128)S(1)}, f32[384,256]{1,0:T(8,128)S(1)}, u32[]{:S(2)}, u32[]{:S(2)}) collective-permute-start(f32[384,256]{1,0:T(8,128)S(1)} %pad_maximum_fusion), channel_id=1, source_target_pairs={{0,1},{1,0},{2,3},{3,2},{4,5},{5,4},{6,7},{7,6},{8,9},{9,8},{10,11... | collective-permute-start | bytes 1179656 | tf_op jit(solution)/shard_map/ppermute | solution.py:428

commit v3 on v2

--- a/solution.py
+++ b/solution.py
@@ -17,6 +17,7 @@
 SB = 8
 NF = SAMP // SF
 NB = SAMP // SB
+ORDER = (0, 3, 1, 2)
 F32 = jnp.float32
 LOG2E = 1.4426950408889634
 LN2 = 0.6931471805599453
@@ -273,25 +274,18 @@
             g_all[j] = g
 
     n = step * SB
+    gout = []
     for j in range(SB):
         g = g_all[step * SB + j]
         gacc[...] += g[:, 0:128] + g[:, 128:256] + g[:, 256:384] + g[:, 384:512]
-        gb = [[jnp.broadcast_to(g[c : c + 1, 128 * t : 128 * t + 128], (8, 128)) for t in range(4)] for c in range(4)]
-        for r in range(0, H, 16):
-            rows = slice(r, r + 16)
-            parts = [None] * 4
-            for t in range(4):
-                lanes = slice(128 * t, 128 * t + 128)
-                h3 = h3h_ref[n + j, rows, lanes].astype(F32) + h3l_ref[n + j, rows, lanes].astype(F32)
-                for c in range(4):
-                    p = jnp.concatenate([h3[0:8] * gb[c][t], h3[8:16] * gb[c][t]], axis=0)
-                    parts[c] = p if parts[c] is None else parts[c] + p
-            for c in range(4):
-                goacc[c, rows] += parts[c]
         gh, gl = split(g)
         gh, gl = gh.astype(F32), gl.astype(F32)
         gk = jnp.concatenate([gh, gl, gh, jnp.zeros((8, RAYS), F32)], axis=0).astype(BF16)
+        g16 = jnp.concatenate([gh, gl], axis=0).astype(BF16)
+        d = mm_nt(jnp.concatenate([g16, g16], axis=1), jnp.concatenate([h3h_ref[n + j], h3l_ref[n + j]], axis=1))
+        gout.append(d[0:8] + d[8:16])
         dh_buf[j] = mm(wo[...], gk)
+    goacc[...] += sum(gout[1:], gout[0])
     sigs = (s3_ref, s2_ref, s1_ref)
     hs = ((h2h_ref, h2l_ref), (h1h_ref, h1l_ref), (fh_ref, fl_ref))
     for i in range(3):
@@ -322,8 +316,7 @@
         gb = jnp.broadcast_to(jnp.sum(gacc[...], axis=1, keepdims=True), (8, 128))
         gb = jnp.sum(jnp.where(lane == sub, gb, F32(0.0)), axis=0, keepdims=True)
         gb = jnp.concatenate([gb, jnp.zeros((1, 128), F32)], axis=1)
-        outw = [jnp.sum(goacc[c].T, axis=0, keepdims=True) * F32(LN2) for c in range(4)]
-        small = jnp.concatenate(outw + hid + [gb], axis=0)
+        small = jnp.concatenate([goacc[0:4] * F32(LN2)] + hid + [gb], axis=0)
         mine_ref[384:392] = small
         other_ref[384:392] = small
 
@@ -338,7 +331,7 @@
         out_shape=[pltpu.VMEM((3, 1, OWN), F32), pltpu.VMEM((392, H), F32), pltpu.VMEM((392, H), F32)],
         scratch_shapes=[
             pltpu.VMEM((SAMP, 8, RAYS), F32), pltpu.VMEM((8, RAYS), F32), pltpu.VMEM((16, 128), F32),
-            pltpu.VMEM((3, H, H), F32), pltpu.VMEM((3, H, 128), F32), pltpu.VMEM((8, 128), F32), pltpu.VMEM((4, H, 128), F32),
+            pltpu.VMEM((3, H, H), F32), pltpu.VMEM((3, H, 128), F32), pltpu.VMEM((8, 128), F32), pltpu.VMEM((8, H), F32),
             pltpu.VMEM((SB, H, RAYS), F32),
         ],
         compiler_params=pltpu.CompilerParams(vmem_limit_bytes=24 * 1024 * 1024),
@@ -349,19 +342,19 @@
 def copies(side, sources, gin, gmid, sem):
     core, chip = where()
     started = []
-    for k in range(4):
+    for n, k in enumerate(ORDER):
         q = lax.rem(chip + 4 - k, 4)
         rows = pl.ds(((core if side == 0 else 1 - core) * 4 + q) * 32, 32)
-        src, base = sources(k)
+        src, base = sources(n)
         for i, dst in enumerate((gin.at[0, rows], gmid.at[0, 0, rows], gmid.at[0, 1, rows])):
-            copy = pltpu.make_async_copy(src.at[pl.ds(base + 32 * i, 32)], dst, sem.at[3 * k + i])
+            copy = pltpu.make_async_copy(src.at[pl.ds(base + 32 * i, 32)], dst, sem.at[3 * n + i])
             copy.start()
             started.append(copy)
     return started
 
 
-def place_own_kernel(done, own1, own2, own3, gin, gmid, gout, ghid, gbout, sem):
-    own = (done, own1, own2, own3)
+def place_own_kernel(done, own_a, own_b, own_c, gin, gmid, gout, ghid, gbout, sem):
+    own = (done, own_a, own_b, own_c)
     started = copies(0, lambda k: (own[k], 0), gin, gmid, sem)
     gout[0] = done[96:100]
     for i in range(3):
@@ -424,7 +417,7 @@
     got = [lax.ppermute(parts[k], "rays", along[k]) for k in range(1, 4)]
     done = parts[0] + got[0] + got[1] + got[2]
     chunk = done[0:96]
-    own = [lax.ppermute(chunk, "rays", along[k]) for k in range(1, 4)]
+    own = [lax.ppermute(chunk, "rays", along[k]) for k in ORDER[1:]]
     sib = lax.ppermute(jnp.concatenate([chunk] + own, axis=0), "rays", swap)
     grad_in, grad_mid, grad_out, grad_hid, grad_bout = place_own(done, own)
     grad_in, grad_mid = place_other(sib, grad_in, grad_mid)

time: 73.7 us -> 72.3 us (0.981)
    ppermute x1, starting transfers between devices: 3.46 us -> 1.27 us  [shards(): sib = lax.ppermute(jnp.concatenate([chunk] + own, axis=0), 'rays', swap)]
    ppermute x3, starting transfers between devices: 1.54 us -> 3.19 us  [shards(): own = [lax.ppermute(chunk, 'rays', along[k]) for k in ORDER[1:]]]
where the time goes in v3:
time: 72.3 us; the launch traced here: 72.2 us
  blocking collectives  23.8 us (33%)
  Pallas kernels  23.6 us (33%)
  waiting for transfers between devices  12 us (17%)
  starting transfers between devices  11.1 us (15%)
  between operations  0.9 us (1%)
    all_to_all x1, blocking collectives, shards(): lax.all_to_all(send.reshape(32, 1, ROWS * 128), 'slab', 0, 0, tiled=True)  23.8 us
    pallas_call x1, Pallas kernels, forward(): pl.pallas_call(lambda *refs: forward_kernel(*refs, delta=delta), grid=(NF...  10.9 us
    pallas_call x1, Pallas kernels, backward(): pl.pallas_call(lambda *refs: backward_kernel(*refs, factor=factor), grid=...  10.4 us
    ppermute x3, waiting for transfers between devices, shards(): got = [lax.ppermute(parts[k], 'rays', along[k]) for k in range(1, 4)]  5.99 us
    ppermute x3, waiting for transfers between devices, shards(): own = [lax.ppermute(chunk, 'rays', along[k]) for k in ORDER[1:]]  4.67 us
    ppermute x3, starting transfers between devices, shards(): got = [lax.ppermute(parts[k], 'rays', along[k]) for k in range(1, 4)]  4.36 us
    ppermute x3, starting transfers between devices, shards(): own = [lax.ppermute(chunk, 'rays', along[k]) for k in ORDER[1:]]  3.19 us
    ppermute x1, starting transfers between devices, shards(): total = mine + lax.ppermute(other, 'rays', swap)  2.27 us
  transfers between devices with their start and end apart: 8, of which 5 were waited for; matrix products, arithmetic and copies ran while one was open for 1% of the time, Pallas kernels for 2%

profile of v3, /device:TPU:1, one launch (start us, length us, event | category | flops | bytes accessed | tf_op | source)
XLA Modules:
  0.0 72.2 jit_solution(13828620911522621103)
XLA Ops:
  0.6 10.9 %fwd.1 = (f32[544,128]{1,0:T(8,128)}, bf16[2,256,768]{2,1,0:T(8,128)(2,1)S(1)}, bf16[256,32]{1,0:T(8,128)(2,1)S(1)}, f32[8,8,512]{2,1,0:T(8,128)S(1)}, bf16[8,25...) custom-call(f32[6,1,512]{2,1,0:T(1,128)} %refs_0_.1, ...), custom_call_target="tpu_custom_call" | custom-call | tf_op jit(solution)/shard_map/fwd/pallas_call | solution.py:194
  11.6 23.8 %all_to_all.5 = f32[32,1,2176]{2,1,0:T(1,128)S(1)} all-to-all(f32[32,1,2176]{2,1,0:T(1,128)} %bitcast.6), channel_id=1, replica_groups=mesh['slab'=32,'rays'=8] {'slab'}, dimensions={0} | all-to-all | bytes 557056 | tf_op jit(solution)/shard_map/all_to_all | solution.py:410
  35.4 10.4 %bwd.1 = (f32[3,1,16]{2,1,0:T(1,128)S(1)}, f32[392,256]{1,0:T(8,128)S(1)}, f32[392,256]{1,0:T(8,128)S(1)}) custom-call(f32[544,128]{1,0:T(8,128)S(1)} %bitcast.5, bf16[2,256,768]{2,1,0:T(8,128)(2,1)S(1)} %get-tuple-element.32.refs_1_, bf16[256,32]{1,0:T(8,128)(2,1)S(1)} %get-tuple-element.33.refs_2_, f32[8,8,512]{2,1,0:T(8,128)S(1)} %get-tuple-element.34.refs_3_, ...), custom_call_target="tpu_custom_call" | custom-call | tf_op jit(solution)/shard_map/bwd/pallas_call | solution.py:326
  45.7 2.3 %collective-permute-start = (f32[392,256]{1,0:T(8,128)S(1)}, f32[392,256]{1,0:T(8,128)S(1)}, u32[]{:S(2)}, u32[]{:S(2)}) collective-permute-start(f32[392,256]{1,0:T(8,128)S(1)} %get-tuple-element.48), channel_id=1, source_target_pairs={{0,1},{1,0},{2,3},{3,2},{4,5},{5,4},{6,7},{7,6},{8,9},{9,8},{10,11... | collective-permute-start | bytes 1204232 | tf_op jit(solution)/shard_map/ppermute | solution.py:414
  48.0 1.4 %collective-permute-done = f32[392,256]{1,0:T(8,128)S(1)} collective-permute-done((f32[392,256]{1,0:T(8,128)S(1)}, f32[392,256]{1,0:T(8,128)S(1)}, u32[]{:S(2)}, u32[]{:S(2)}) %collective-permute-start) | collective-permute-done | bytes 401440 | tf_op jit(solution)/shard_map/ppermute | solution.py:414
  49.4 0.1 add.12
  49.5 2.6 %collective-permute-start.3 = (f32[104,256]{1,0:T(8,128)S(1)}, f32[104,256]{1,0:T(8,128)S(1)}, u32[]{:S(2)}, u32[]{:S(2)}) collective-permute-start(f32[104,256]{1,0:T(8,128)S(1)} %concatenate.20), channel_id=1, source_target_pairs={{0,6},{1,7},{2,0},{3,1},{4,2},{5,3},{6,4},{7,5},{8,14},{9,15},{10,... | collective-permute-start | bytes 319496 | tf_op jit(solution)/shard_map/ppermute | solution.py:417
  52.1 0.1 collective-permute-start.1
  52.2 1.7 %collective-permute-start.2 = (f32[104,256]{1,0:T(8,128)S(1)}, f32[104,256]{1,0:T(8,128)S(1)}, u32[]{:S(2)}, u32[]{:S(2)}) collective-permute-start(f32[104,256]{1,0:T(8,128)S(1)} %get-tuple-element.60), channel_id=1, source_target_pairs={{0,4},{1,5},{2,6},{3,7},{4,0},{5,1},{6,2},{7,3},{8,12},{9,13},{10,... | collective-permute-start | bytes 319496 | tf_op jit(solution)/shard_map/ppermute | solution.py:417
  53.9 0.1 collective-permute-done.3
  54.0 5.9 %collective-permute-done.1 = f32[104,256]{1,0:T(8,128)S(1)} collective-permute-done((f32[104,256]{1,0:T(8,128)S(1)}, f32[104,256]{1,0:T(8,128)S(1)}, u32[]{:S(2)}, u32[]{:S(2)}) %collective-permute-start.1) | collective-permute-done | bytes 106528 | tf_op jit(solution)/shard_map/ppermute | solution.py:417
  59.9 0.0 collective-permute-done.2
  59.9 0.5 collective-permute-start.6
  60.4 0.4 collective-permute-start.5
  60.8 2.3 %collective-permute-start.4 = (f32[96,256]{1,0:T(8,128)S(1)}, f32[96,256]{1,0:T(8,128)S(1)}, u32[]{:S(2)}, u32[]{:S(2)}) collective-permute-start(f32[96,256]{1,0:T(8,128)S(1)} %slice.26), channel_id=1, source_target_pairs={{0,6},{1,7},{2,0},{3,1},{4,2},{5,3},{6,4},{7,5},{8,14},{9,15},{10,... | collective-permute-start | bytes 294920 | tf_op jit(solution)/shard_map/ppermute | solution.py:420
  63.1 2.2 %collective-permute-done.6.own_c = f32[96,256]{1,0:T(8,128)S(1)} collective-permute-done((f32[96,256]{1,0:T(8,128)S(1)}, f32[96,256]{1,0:T(8,128)S(1)}, u32[]{:S(2)}, u32[]{:S(2)}) %collective-permute-start.6) | collective-permute-done | bytes 98336 | tf_op jit(solution)/shard_map/ppermute | solution.py:420
  65.3 2.5 %collective-permute-done.5.own_b = f32[96,256]{1,0:T(8,128)S(1)} collective-permute-done((f32[96,256]{1,0:T(8,128)S(1)}, f32[96,256]{1,0:T(8,128)S(1)}, u32[]{:S(2)}, u32[]{:S(2)}) %collective-permute-start.5) | collective-permute-done | bytes 98336 | tf_op jit(solution)/shard_map/ppermute | solution.py:420
  67.8 0.0 collective-permute-done.4.own_a
  67.8 1.3 %collective-permute-start.7 = (f32[384,256]{1,0:T(8,128)S(1)}, f32[384,256]{1,0:T(8,128)S(1)}, u32[]{:S(2)}, u32[]{:S(2)}) collective-permute-start(f32[384,256]{1,0:T(8,128)S(1)} %pad_maximum_fusion), channel_id=1, source_target_pairs={{0,1},{1,0},{2,3},{3,2},{4,5},{5,4},{6,7},{7,6},{8,9},{9,8},{10,11... | collective-permute-start | bytes 1179656 | tf_op jit(solution)/shard_map/ppermute | solution.py:421
  69.1 0.6 copy.21
  69.7 1.4 %place_own.1 = (f32[1,256,256]{2,1,0:T(8,128)}, f32[1,2,256,256]{3,2,1,0:T(8,128)}, f32[1,4,256]{2,1,0:T(4,128)}, f32[3,1,256]{2,1,0:T(1,128)}, f32[1,4]{1,0:T(1,128)}) custom-call(f32[104,256]{1,0:T(8,128)S(1)} %fusion.2.done, f32[96,256]{1,0:T(8,128)S(1)} %collective-permute-done.4.own_a, f32[96,256]{1,0:T(8,128)S(1)} %collective-permute-done.5.own_b, ...), custom_call_target="tpu_custom_call" | custom-call | tf_op jit(solution)/shard_map/place_own/pallas_call | solution.py:378
  71.1 0.0 collective-permute-done.7.sib
  71.1 0.9 %place_other.1 = (f32[1,256,256]{2,1,0:T(8,128)}, f32[1,2,256,256]{3,2,1,0:T(8,128)}) custom-call(f32[384,256]{1,0:T(8,128)S(1)} %collective-permute-done.7.sib, f32[1,256,256]{2,1,0:T(8,128)} %get-tuple-element.49.gin_in, f32[1,2,256,256]{3,2,1,0:T(8,128)} %get-tuple-element.50.gmid_in), custom_call_target="tpu_custom_call", output_to_operand_aliasing={{0}: (1, {}), {1}: (2, {})} | custom-call | tf_op jit(solution)/shard_map/place_other/pallas_call | solution.py:390
  (7 shorter events, 0.1 us)
Async XLA Ops:
  45.7 3.6 %collective-permute-start = (f32[392,256]{1,0:T(8,128)S(1)}, f32[392,256]{1,0:T(8,128)S(1)}, u32[]{:S(2)}, u32[]{:S(2)}) collective-permute-start(f32[392,256]{1,0:T(8,128)S(1)} %get-tuple-element.48), channel_id=1, source_target_pairs={{0,1},{1,0},{2,3},{3,2},{4,5},{5,4},{6,7},{7,6},{8,9},{9,8},{10,11... | collective-permute-start | bytes 1204232 | tf_op jit(solution)/shard_map/ppermute | solution.py:414
  49.5 4.5 %collective-permute-start.3 = (f32[104,256]{1,0:T(8,128)S(1)}, f32[104,256]{1,0:T(8,128)S(1)}, u32[]{:S(2)}, u32[]{:S(2)}) collective-permute-start(f32[104,256]{1,0:T(8,128)S(1)} %concatenate.20), channel_id=1, source_target_pairs={{0,6},{1,7},{2,0},{3,1},{4,2},{5,3},{6,4},{7,5},{8,14},{9,15},{10,... | collective-permute-start | bytes 319496 | tf_op jit(solution)/shard_map/ppermute | solution.py:417
  52.1 7.8 %collective-permute-start.1 = (f32[104,256]{1,0:T(8,128)S(1)}, f32[104,256]{1,0:T(8,128)S(1)}, u32[]{:S(2)}, u32[]{:S(2)}) collective-permute-start(f32[104,256]{1,0:T(8,128)S(1)} %get-tuple-element.59), channel_id=1, source_target_pairs={{0,2},{1,3},{2,4},{3,5},{4,6},{5,7},{6,0},{7,1},{8,10},{9,11},{10,... | collective-permute-start | bytes 319496 | tf_op jit(solution)/shard_map/ppermute | solution.py:417
  52.2 7.7 %collective-permute-start.2 = (f32[104,256]{1,0:T(8,128)S(1)}, f32[104,256]{1,0:T(8,128)S(1)}, u32[]{:S(2)}, u32[]{:S(2)}) collective-permute-start(f32[104,256]{1,0:T(8,128)S(1)} %get-tuple-element.60), channel_id=1, source_target_pairs={{0,4},{1,5},{2,6},{3,7},{4,0},{5,1},{6,2},{7,3},{8,12},{9,13},{10,... | collective-permute-start | bytes 319496 | tf_op jit(solution)/shard_map/ppermute | solution.py:417
  59.9 5.4 %collective-permute-start.6 = (f32[96,256]{1,0:T(8,128)S(1)}, f32[96,256]{1,0:T(8,128)S(1)}, u32[]{:S(2)}, u32[]{:S(2)}) collective-permute-start(f32[96,256]{1,0:T(8,128)S(1)} %slice.26), channel_id=1, source_target_pairs={{0,4},{1,5},{2,6},{3,7},{4,0},{5,1},{6,2},{7,3},{8,12},{9,13},{10,... | collective-permute-start | bytes 294920 | tf_op jit(solution)/shard_map/ppermute | solution.py:420
  60.4 7.3 %collective-permute-start.5 = (f32[96,256]{1,0:T(8,128)S(1)}, f32[96,256]{1,0:T(8,128)S(1)}, u32[]{:S(2)}, u32[]{:S(2)}) collective-permute-start(f32[96,256]{1,0:T(8,128)S(1)} %slice.26), channel_id=1, source_target_pairs={{0,2},{1,3},{2,4},{3,5},{4,6},{5,7},{6,0},{7,1},{8,10},{9,11},{10,... | collective-permute-start | bytes 294920 | tf_op jit(solution)/shard_map/ppermute | solution.py:420
  60.8 7.0 %collective-permute-start.4 = (f32[96,256]{1,0:T(8,128)S(1)}, f32[96,256]{1,0:T(8,128)S(1)}, u32[]{:S(2)}, u32[]{:S(2)}) collective-permute-start(f32[96,256]{1,0:T(8,128)S(1)} %slice.26), channel_id=1, source_target_pairs={{0,6},{1,7},{2,0},{3,1},{4,2},{5,3},{6,4},{7,5},{8,14},{9,15},{10,... | collective-permute-start | bytes 294920 | tf_op jit(solution)/shard_map/ppermute | solution.py:420
  67.8 3.3 %collective-permute-start.7 = (f32[384,256]{1,0:T(8,128)S(1)}, f32[384,256]{1,0:T(8,128)S(1)}, u32[]{:S(2)}, u32[]{:S(2)}) collective-permute-start(f32[384,256]{1,0:T(8,128)S(1)} %pad_maximum_fusion), channel_id=1, source_target_pairs={{0,1},{1,0},{2,3},{3,2},{4,5},{5,4},{6,7},{7,6},{8,9},{9,8},{10,11... | collective-permute-start | bytes 1179656 | tf_op jit(solution)/shard_map/ppermute | solution.py:421
